TPU v7x, 32 devices: a whole 2x2x4 slice. The times are simulated.
32 devices in a mesh: dp: 8 (over z, y), tensor: 4 (over x, core).
Axes of the slice: x: 2, y: 2, z: 4, core: 2. Of those that a mesh axis runs over, the one named last changes fastest.
Arguments:
- out_grad: bfloat16 [2048, 1024], P('dp'), may hold values from -0.29882812 to 0.29882812
- hidden: bfloat16 [2048, 28672], P('dp', 'tensor'), may hold values from -60 to 60
- momentum: float32 [1024, 28672], P('dp', 'tensor'), may hold values from -48 to 48
- second: float32 [1024], P('dp'), may hold values from 0.01 to 0.2
Outputs:
- update: bfloat16 [1024, 28672], P('dp', 'tensor')
- momentum_out: float32 [1024, 28672], P('dp', 'tensor')
- second_out: float32 [1024], P('dp')
All inputs are finite; a program needn't handle non-finite values.
Results may differ from a plain program's by a relative error of at most 0.035.
Values may be sent and summed in bfloat16 or wider, within the bound.
A program may use at most 128 MiB of HBM per device.

v0:
```python
import functools

import jax
import jax.numpy as jnp
from jax import lax
from jax.experimental import pallas as pl
from jax.experimental.pallas import tpu as pltpu
from jax.sharding import PartitionSpec as P

ITERS = 3
quintic_a = 3.4445
quintic_b = -4.775
quintic_c = 2.0315
beta_one = 0.95
beta_two = 0.95

MESH = pl.DeviceIdType.MESH
F32 = jnp.float32
BF16 = jnp.bfloat16


def line_split(n_dp):
    ny = 1
    while ny * ny * 4 <= n_dp and n_dp % (ny * 2) == 0:
        ny *= 2
    return n_dp // ny, ny


def exact_dot(a, b):
    return jnp.dot(a, b, preferred_element_type=F32, precision=lax.Precision.HIGHEST)


def kernel(
    nz, ny, nt, n_chunks, ff,
    og_hbm, h_hbm, mom_hbm, sec_ref,
    x, mom, final_ref, secout_ref,
    h, ograw, og_t, rr, rl, sr, sl, gram, norm, g_all,
    h_sem, og_sem, y_send, og_send, rr_sem, rl_sem, sr_sem, sl_sem, mom_sem,
    g_send, g_recv,
):
    tokens = h_hbm.shape[0]
    rows, width = x.shape[1], x.shape[2]
    d = lax.axis_index("dp")
    t = lax.axis_index("tensor")
    z, y = d // ny, lax.rem(d, ny)

    def at_y(k):
        return (z * ny + lax.rem(y + k, ny), t)

    def at_z(step):
        return (d + step * ny, t)

    def at_t(k):
        return (d, lax.rem(t + k, nt))

    barrier = pltpu.get_barrier_semaphore()
    for k in range(1, ny):
        pl.semaphore_signal(barrier, inc=1, device_id=at_y(k), device_id_type=MESH)
    for k in range(1, nt):
        pl.semaphore_signal(barrier, inc=1, device_id=at_t(k), device_id_type=MESH)

    @pl.when(z > 0)
    def _():
        pl.semaphore_signal(barrier, inc=1, device_id=at_z(-1), device_id_type=MESH)

    @pl.when(z < nz - 1)
    def _():
        pl.semaphore_signal(barrier, inc=1, device_id=at_z(1), device_id_type=MESH)

    mine = pl.ds(pl.multiple_of(y * tokens, tokens), tokens)

    def columns(c):
        return pl.ds(pl.multiple_of(c * width, width), width)

    ends = jnp.minimum(z, 1) + jnp.minimum(nz - 1 - z, 1)
    pl.semaphore_wait(barrier, (ny - 1) + (nt - 1) + ends)

    def far_first(i):
        return jnp.where(z * 2 < nz, nz - 1 - i, i)

    def og_sends(i):
        j = far_first(i)
        for k in range(1, ny):
            peer = lax.rem(y + k, ny)
            cols = pl.ds(pl.multiple_of((j * ny + peer) * rows, rows), rows)
            pltpu.make_async_remote_copy(
                og_hbm.at[:, cols], ograw.at[y, j], og_send.at[k - 1], og_sem.at[y, j],
                device_id=at_y(k), device_id_type=MESH,
            ).start()

    def y_sends(c, carry):
        for k in range(1, ny):
            pltpu.make_async_remote_copy(
                h_hbm.at[:, columns(c)], h.at[c, mine], y_send.at[k - 1], h_sem.at[y, c],
                device_id=at_y(k), device_id_type=MESH,
            ).start()
        return carry

    og_sends(0)
    y_sends(0, 0)
    for i in range(1, nz):
        og_sends(i)
    lax.fori_loop(1, n_chunks, y_sends, 0)

    for j in range(nz):
        cols = pl.ds(pl.multiple_of((j * ny + y) * rows, rows), rows)
        pltpu.make_async_copy(og_hbm.at[:, cols], ograw.at[y, j], og_sem.at[y, j]).start()

    def own_load(c, carry):
        pltpu.make_async_copy(h_hbm.at[:, columns(c)], h.at[c, mine], h_sem.at[y, c]).start()
        return carry

    lax.fori_loop(0, n_chunks, own_load, 0)

    def mom_load(c, carry):
        pltpu.make_async_copy(mom_hbm.at[:, columns(c)], mom.at[c], mom_sem).start()
        return carry

    lax.fori_loop(0, n_chunks, mom_load, 0)
    gram[...] = jnp.zeros_like(gram)
    norm[...] = jnp.zeros_like(norm)
    pltpu.make_async_copy(mom, mom, mom_sem).wait()

    def prepare(j):
        for k in range(ny):
            pltpu.make_async_copy(ograw.at[k, j], ograw.at[k, j], og_sem.at[k, j]).wait()
            og_t[j, :, k * tokens : (k + 1) * tokens] = ograw[k, j].T

    def partial(j, c):
        return jnp.dot(og_t[j], h[c], preferred_element_type=F32)

    def send_on(j, c, slot, first, recv, recv_sem, send, send_sem, step):
        own = partial(j, c)

        @pl.when(first)
        def _():
            send[slot, c] = own.astype(BF16)

        @pl.when(jnp.logical_not(first))
        def _():
            pltpu.make_async_copy(recv.at[slot, c], recv.at[slot, c], recv_sem.at[slot, c]).wait()
            send[slot, c] = (own + recv[slot, c].astype(F32)).astype(BF16)

        pltpu.make_async_remote_copy(
            send.at[slot, c], recv.at[slot, c], send_sem.at[slot], recv_sem.at[slot, c],
            device_id=at_z(step), device_id_type=MESH,
        ).start()

    reach = jnp.maximum(z, nz - 1 - z)

    def step(s, carry):
        @pl.when(s < n_chunks)
        def _():
            for k in range(ny):
                block = h.at[s, pl.ds(k * tokens, tokens)]
                pltpu.make_async_copy(block, block, h_sem.at[k, s]).wait()

        right = s - z

        @pl.when(jnp.logical_and(right >= 0, right < n_chunks))
        def _():
            for j in range(nz - 1, 0, -1):
                @pl.when(z < j)
                def _():
                    @pl.when(s == 0)
                    def _():
                        prepare(j)

                    send_on(j, right, j - 1, z == 0, rr, rr_sem, sr, sr_sem, 1)

        left = s - (nz - 1 - z)

        @pl.when(jnp.logical_and(left >= 0, left < n_chunks))
        def _():
            for j in range(nz - 1):
                @pl.when(z > j)
                def _():
                    @pl.when(s == 0)
                    def _():
                        prepare(j)

                    send_on(j, left, j, z == nz - 1, rl, rl_sem, sl, sl_sem, -1)

        for j in range(nz):
            inner = jnp.logical_and(z > 0, z < nz - 1)

            @pl.when(jnp.logical_and(s == 0, jnp.logical_or(inner, z == j)))
            def _():
                prepare(j)

        c = s - reach

        @pl.when(jnp.logical_and(c >= 0, c < n_chunks))
        def _():
            x_grad = norm.at[1]
            x_grad[...] = partial(z, c)

            @pl.when(z > 0)
            def _():
                pltpu.make_async_copy(rr.at[z - 1, c], rr.at[z - 1, c], rr_sem.at[z - 1, c]).wait()
                x_grad[...] += rr[z - 1, c].astype(F32)

            @pl.when(z < nz - 1)
            def _():
                pltpu.make_async_copy(rl.at[z, c], rl.at[z, c], rl_sem.at[z, c]).wait()
                x_grad[...] += rl[z, c].astype(F32)

            grad = x_grad[...]
            momentum_out = beta_one * mom[c] + grad
            nesterov = grad + beta_one * momentum_out
            mom[c] = momentum_out
            panel = nesterov.astype(BF16)
            x[c] = panel
            norm[0] += nesterov * nesterov
            gram[...] += lax.dot_general(
                panel, panel, (((1,), (1,)), ((), ())), preferred_element_type=F32
            )

        return carry

    lax.fori_loop(0, n_chunks + nz - 1, step, 0)

    g_all[t, :rows] = gram[...]
    total = jnp.sum(jnp.sum(norm[0], axis=0, keepdims=True), axis=1, keepdims=True)
    g_all[t, rows:] = jnp.broadcast_to(total, (8, rows))
    for k in range(1, nt):
        pltpu.make_async_remote_copy(
            g_all.at[t], g_all.at[t], g_send.at[k - 1], g_recv.at[t],
            device_id=at_t(k), device_id_type=MESH,
        ).start()
    for k in range(nt):
        @pl.when(k != t)
        def _():
            pltpu.make_async_copy(g_all.at[k], g_all.at[k], g_recv.at[k]).wait()
    summed = g_all[0]
    for k in range(1, nt):
        summed = summed + g_all[k]
    inverse = 1.0 / (jnp.sqrt(summed[rows : rows + 1]) + 1e-07)
    current = summed[:rows] * inverse * inverse
    eye = (
        lax.broadcasted_iota(jnp.int32, (rows, rows), 0)
        == lax.broadcasted_iota(jnp.int32, (rows, rows), 1)
    ).astype(F32)
    map_all = None
    for iteration in range(ITERS):
        square = exact_dot(current, current)
        map_one = quintic_a * eye + quintic_b * current + quintic_c * square
        map_all = map_one if map_all is None else exact_dot(map_one, map_all)
        mapped = exact_dot(map_one, current)
        if iteration < ITERS - 1:
            current = exact_dot(mapped, map_one)
    energy = jnp.sum(mapped * map_one, axis=0, keepdims=True)
    second_out = beta_two * sec_ref[...] + (1.0 - beta_two) * energy
    secout_ref[...] = second_out
    scale = jnp.sqrt(ff / second_out) * inverse
    final = jnp.sum(eye * scale, axis=1, keepdims=True) * map_all
    final_ref[...] = final

    for k in range(1, ny):
        pltpu.make_async_copy(ograw.at[0], ograw.at[0], og_send.at[k - 1]).wait()
        blocks = h.at[:, pl.ds(0, tokens)]
        pltpu.make_async_copy(blocks, blocks, y_send.at[k - 1]).wait()
    for j in range(1, nz):
        @pl.when(z < j)
        def _():
            pltpu.make_async_copy(sr.at[j - 1], sr.at[j - 1], sr_sem.at[j - 1]).wait()
    for j in range(nz - 1):
        @pl.when(z > j)
        def _():
            pltpu.make_async_copy(sl.at[j], sl.at[j], sl_sem.at[j]).wait()
    for k in range(1, nt):
        pltpu.make_async_copy(g_all.at[0], g_all.at[0], g_send.at[k - 1]).wait()


def write_kernel(n_chunks, x, mom, final_ref, sec_ref, upd_hbm, momout_hbm, secout_ref, out, mom_sem, upd_sem):
    width = x.shape[2]

    def columns(c):
        return pl.ds(pl.multiple_of(c * width, width), width)

    high = final_ref[...].astype(BF16)
    low = (final_ref[...] - high.astype(F32)).astype(BF16)
    secout_ref[...] = sec_ref[...]

    def finish(c, carry):
        pltpu.make_async_copy(mom.at[c], momout_hbm.at[:, columns(c)], mom_sem).start()
        panel = x[c]
        result = jnp.dot(high, panel, preferred_element_type=F32)
        result += jnp.dot(low, panel, preferred_element_type=F32)
        out[c] = result.astype(BF16)
        pltpu.make_async_copy(out.at[c], upd_hbm.at[:, columns(c)], upd_sem).start()
        return carry

    lax.fori_loop(0, n_chunks, finish, 0)
    pltpu.make_async_copy(mom, mom, mom_sem).wait()
    pltpu.make_async_copy(out, out, upd_sem).wait()


def body(nz, ny, nt, out_grad, hidden, momentum, second):
    tokens, cols = hidden.shape
    rows = momentum.shape[0]
    width = 256 if cols % 256 == 0 else 128
    n_chunks = cols // width
    dma = pltpu.SemaphoreType.DMA
    anywhere = pl.BlockSpec(memory_space=pltpu.HBM)
    vmem = pl.BlockSpec(memory_space=pltpu.VMEM)
    hops = (nz - 1, n_chunks)
    panel, mom, final, second_out = pl.pallas_call(
        functools.partial(kernel, nz, ny, nt, n_chunks, float(cols * nt)),
        out_shape=(
            jax.ShapeDtypeStruct((n_chunks, rows, width), BF16),
            jax.ShapeDtypeStruct((n_chunks, rows, width), F32),
            jax.ShapeDtypeStruct((rows, rows), F32),
            jax.ShapeDtypeStruct((1, rows), F32),
        ),
        in_specs=[anywhere, anywhere, anywhere, vmem],
        out_specs=(vmem, vmem, vmem, vmem),
        scratch_shapes=[
            pltpu.VMEM((n_chunks, ny * tokens, width), BF16),
            pltpu.VMEM((ny, nz, tokens, rows), BF16),
            pltpu.VMEM((nz, rows, ny * tokens), BF16),
            pltpu.VMEM(hops + (rows, width), BF16),
            pltpu.VMEM(hops + (rows, width), BF16),
            pltpu.VMEM(hops + (rows, width), BF16),
            pltpu.VMEM(hops + (rows, width), BF16),
            pltpu.VMEM((rows, rows), F32),
            pltpu.VMEM((2, rows, width), F32),
            pltpu.VMEM((nt, rows + 8, rows), F32),
            dma((ny, n_chunks)),
            dma((ny, nz)),
            dma((max(ny - 1, 1),)),
            dma((max(ny - 1, 1),)),
            dma(hops),
            dma(hops),
            dma((nz - 1,)),
            dma((nz - 1,)),
            dma,
            dma((max(nt - 1, 1),)),
            dma((nt,)),
        ],
        compiler_params=pltpu.CompilerParams(
            collective_id=0, has_side_effects=True, vmem_limit_bytes=47 * 1024 * 1024
        ),
        name="normuon",
    )(out_grad, hidden, momentum, second.reshape(1, rows))
    update, momentum_out, second_out = pl.pallas_call(
        functools.partial(write_kernel, n_chunks),
        out_shape=(
            jax.ShapeDtypeStruct((rows, cols), BF16),
            jax.ShapeDtypeStruct((rows, cols), F32),
            jax.ShapeDtypeStruct((1, rows), F32),
        ),
        in_specs=[vmem] * 4,
        out_specs=(anywhere, anywhere, vmem),
        scratch_shapes=[pltpu.VMEM((n_chunks, rows, width), BF16), dma, dma],
        compiler_params=pltpu.CompilerParams(vmem_limit_bytes=16 * 1024 * 1024),
        name="write_results",
    )(panel, mom, final, second_out)
    return update, momentum_out, second_out.reshape(rows)


def solution(mesh):
    nz, ny = line_split(mesh.shape["dp"])
    placed = (P("dp", None), P("dp", "tensor"), P("dp", "tensor"), P("dp"))
    return jax.shard_map(
        functools.partial(body, nz, ny, mesh.shape["tensor"]),
        mesh=mesh,
        in_specs=placed,
        out_specs=(P("dp", "tensor"), P("dp", "tensor"), P("dp")),
        check_vma=False,
    )
```

profile of v0, /device:TPU:0, one launch (start us, length us, event | category | flops | bytes accessed | tf_op | source)
XLA Modules:
  0.0 154.6 jit_solution(18349574715474287488)
XLA Ops:
  0.6 0.0 copy-start
  0.6 1.0 copy-done
  1.7 0.0 copy-start.1
  1.7 0.7 copy-done.1
  2.3 146.1 %normuon.1 = (bf16[28,128,256]{2,1,0:T(8,128)(2,1)S(1)}, f32[28,128,256]{2,1,0:T(8,128)S(1)}, f32[128,128]{1,0:T(8,128)S(1)}, f32[1,128]{1,0:T(1,128)S(1)}) custom-call(bf16[256,1024]{1,0:T(8,128)(2,1)S(1)} %copy-done, bf16[256,7168]{1,0:T(8,128)(2,1)} %h_hbm.1, f32[128,7168]{1,0:T(8,128)} %mom_hbm.1, f32[1,128]{1,0:T(1,128)S(1)} %bitcast.2), custom_call_target="tpu_custom_call" | custom-call | tf_op jit(solution)/shard_map/normuon/pallas_call | solution.py:308
  148.5 6.1 %write_results.1 = (bf16[128,7168]{1,0:T(8,128)(2,1)}, f32[128,7168]{1,0:T(8,128)}, f32[1,128]{1,0:T(1,128)}) custom-call(bf16[28,128,256]{2,1,0:T(8,128)(2,1)S(1)} %get-tuple-element.10.x, f32[28,128,256]{2,1,0:T(8,128)S(1)} %get-tuple-element.11.mom, f32[128,128]{1,0:T(8,128)S(1)} %get-tuple-element.12.final_ref, f32[1,128]{1,0:T(1,128)S(1)} %get-tuple-element.13.sec_ref), custom_call_target="tpu_custom_call" | custom-call | tf_op jit(solution)/shard_map/write_results/pallas_call | solution.py:346
Async XLA Ops:
  0.6 1.0 copy-start
  1.7 0.7 copy-start.1
where the time goes:
time: 155 us
  Pallas kernels  152 us (98%)
  local copies, waits for them, and re-layouts  1.69 us (1%)
    pallas_call x1, Pallas kernels, body(): pl.pallas_call(functools.partial(kernel, nz, ny, nt, n_chunks, float(cols...  146 us
    pallas_call x1, Pallas kernels, body(): pl.pallas_call(functools.partial(write_kernel, n_chunks), out_shape=(jax....  6.11 us

commit v1 on v0

v1 whole, which is shorter than its diff:
```python
import functools

import jax
import jax.numpy as jnp
from jax import lax
from jax.experimental import pallas as pl
from jax.experimental.pallas import tpu as pltpu
from jax.sharding import PartitionSpec as P

ITERS = 3
quintic_a = 3.4445
quintic_b = -4.775
quintic_c = 2.0315
beta_one = 0.95
beta_two = 0.95

MESH = pl.DeviceIdType.MESH
F32 = jnp.float32
BF16 = jnp.bfloat16


def line_split(n_dp):
    ny = 1
    while ny * ny * 4 <= n_dp and n_dp % (ny * 2) == 0:
        ny *= 2
    return n_dp // ny, ny


def exact_dot(a, b):
    return jnp.dot(a, b, preferred_element_type=F32, precision=lax.Precision.HIGHEST)


def kernel(
    nz, ny, nt, n, ff,
    og_hbm, h_hbm, mom_hbm, sec_ref,
    x, mom, final_ref, secout_ref,
    h, ograw, og_t, recv, send, fin, acc, gram, norm, g_all,
    h_sem, og_sem, og_own, recv_sem, fin_sem, mom_sem,
    hy_send, end_send, fwd_send, og_send, ogx_send, ogc_send, s_send, g_send, g_recv,
):
    tokens, part = h_hbm.shape[0], h_hbm.shape[1] // ny
    rows, width = x.shape[1], x.shape[2]
    group = ny * rows
    tau = tokens // nt
    nx = nt // 2
    slots = 2 * ny
    half = nz // 2
    ahead, end_ahead, lag, fin_lag = 6, 3, 2, 2
    d = lax.axis_index("dp")
    t = lax.axis_index("tensor")
    z, y = d // ny, lax.rem(d, ny)
    tx, core = t // 2, lax.rem(t, 2)
    lower = z * 2 < nz
    zm = jnp.where(lower, z, nz - 1 - z)
    toward = jnp.where(lower, 1, -1)
    is_end = zm == 0

    def mirrored(jm):
        return jnp.where(lower, jm, nz - 1 - jm)

    def far_slot(j):
        return jnp.where(lower, j + 1, j)

    def near_slot(j):
        return jnp.where(lower, j, j + 1)

    def at(zz, yy):
        return (zz * ny + yy, t)

    def at_y(k):
        return at(z, lax.rem(y + k, ny))

    def at_t(tt):
        return (d, tt)

    def when(cond, fn):
        if isinstance(cond, bool):
            if cond:
                fn()
        else:
            pl.when(cond)(fn)

    def remote(src, dst, send_sem, recv_sem, device):
        pltpu.make_async_remote_copy(
            src, dst, send_sem, recv_sem, device_id=device, device_id_type=MESH
        ).start()

    def arrived(ref, sem):
        pltpu.make_async_copy(ref, ref, sem).wait()

    def block(i, size):
        return pl.ds(pl.multiple_of(i * size, size), size)

    def columns(p, c):
        return block(p * n + c, width)

    inner_z = 1 if half == 2 else zm
    z_end = jnp.where(lower, 0, nz - 1)

    barrier = pltpu.get_barrier_semaphore()

    def hello(device):
        pl.semaphore_signal(barrier, inc=1, device_id=device, device_id_type=MESH)

    for k in range(1, ny):
        hello(at_y(k))
    for k in range(1, nt):
        hello(at_t(lax.rem(t + k, nt)))

    @pl.when(is_end)
    def _():
        for k in range(ny):
            hello(at(z + toward, k))

    @pl.when(jnp.logical_not(is_end))
    def _():
        hello(at(z + toward, y))

        def ends():
            for k in range(ny):
                hello(at(z_end, k))

        def next_in():
            hello(at(z - toward, y))

        if half == 2:
            ends()
        else:
            pl.when(zm == 1)(ends)
            pl.when(zm > 1)(next_in)

    greeted = (ny - 1) + (nt - 1)
    pl.semaphore_wait(
        barrier,
        greeted + jnp.where(zm == 0, ny, 0) + jnp.where(zm == 1, ny + 1, 0) + jnp.where(zm > 1, 2, 0),
    )

    piece = block(t, tau)

    def rows_of(j):
        return block(j, group)

    def y_send(c):
        for k in range(1, ny):
            p = lax.rem(y + k, ny)
            remote(
                h_hbm.at[:, columns(p, c)], h.at[c, block(y, tokens)],
                hy_send.at[k - 1], h_sem.at[y, c], at_y(k),
            )

    def mom_load(c, carry):
        pltpu.make_async_copy(mom_hbm.at[:, block(c, width)], mom.at[c], mom_sem).start()
        return carry

    def process(q, grad):
        momentum_out = beta_one * mom[q] + grad
        nesterov = grad + beta_one * momentum_out
        mom[q] = momentum_out
        panel = nesterov.astype(BF16)
        x[q] = panel
        norm[...] += nesterov * nesterov
        gram[...] += lax.dot_general(
            panel, panel, (((1,), (1,)), ((), ())), preferred_element_type=F32
        )

    def process_fin(p, c):
        arrived(fin.at[p, c], fin_sem.at[p, c])
        process(p * n + c, fin[p, c].astype(F32))

    @pl.when(is_end)
    def _():
        z_in = z + toward

        def og_to_inner(i):
            j = mirrored(nz - 1 - i)
            for k in range(ny):
                remote(
                    og_hbm.at[piece, rows_of(j)], ograw.at[ny + y, piece, rows_of(j)],
                    og_send.at[k], og_sem.at[ny + y, j, t], at(z_in, lax.rem(y + k, ny)),
                )

        def own_to_inner(c):
            remote(
                h_hbm.at[:, columns(y, c)], h.at[c, block(ny + y, tokens)],
                end_send, h_sem.at[ny + y, c], at(z_in, y),
            )

        og_to_inner(0)
        for c in range(min(2, n)):
            y_send(c)
        for i in range(1, nz):
            og_to_inner(i)
            if i <= min(end_ahead, n):
                own_to_inner(i - 1)
        for c in range(min(nz - 1, end_ahead, n), min(end_ahead, n)):
            own_to_inner(c)

        def rest(c, carry):
            y_send(c)
            return carry

        lax.fori_loop(min(2, n), n, rest, 0)
        lax.fori_loop(0, ny * n, mom_load, 0)
        gram[...] = jnp.zeros_like(gram)
        norm[...] = jnp.zeros_like(norm)

        def forward(c, carry):
            for k in range(1, ny):
                p = lax.rem(y + k, ny)
                arrived(h.at[c, block(p, tokens)], h_sem.at[p, c])
                remote(
                    h.at[c, block(p, tokens)], h.at[c, block(ny + p, tokens)],
                    fwd_send.at[k - 1], h_sem.at[ny + p, c], at(z_in, y),
                )

            @pl.when(c + end_ahead < n)
            def _():
                own_to_inner(c + end_ahead)

            return carry

        lax.fori_loop(0, n, forward, 0)
        pltpu.make_async_copy(mom, mom, mom_sem).wait()

        def finish(c, carry):
            for k in range(ny):
                process_fin(lax.rem(y + k, ny), c)
            return carry

        lax.fori_loop(0, n, finish, 0)

    @pl.when(jnp.logical_not(is_end))
    def _():
        near_end = inner_z == 1
        for i in range(nz):
            j = mirrored(nz - 1 - i)
            for k in range(1, ny):
                remote(
                    og_hbm.at[piece, rows_of(j)], ograw.at[y, piece, rows_of(j)],
                    og_send.at[k], og_sem.at[y, j, t], at_y(k),
                )
        for c in range(min(ahead, n)):
            y_send(c)
        pltpu.make_async_copy(og_hbm, ograw.at[y], og_own).start()

        def own_load(c, carry):
            pltpu.make_async_copy(
                h_hbm.at[:, columns(y, c)], h.at[c, block(y, tokens)], h_sem.at[y, c]
            ).start()
            return carry

        lax.fori_loop(0, n, own_load, 0)
        lax.fori_loop(0, ny * n, mom_load, 0)
        gram[...] = jnp.zeros_like(gram)
        norm[...] = jnp.zeros_like(norm)
        if half > 2:
            @pl.when(zm > 1)
            def _():
                h[:, ny * tokens :] = jnp.zeros((n, ny * tokens, width), BF16)
                ograw[ny:] = jnp.zeros((ny,) + ograw.shape[1:], BF16)

        pltpu.make_async_copy(mom, mom, mom_sem).wait()
        pltpu.make_async_copy(og_hbm, ograw.at[y], og_own).wait()

        def each_slot(fn):
            for k in range(1, ny):
                fn(lax.rem(y + k, ny))

            def from_end():
                for p in range(ny):
                    fn(ny + p)

            when(near_end, from_end)

        def og_piece(slot, tt, j):
            return ograw.at[slot, block(tt, tau), rows_of(j)]

        def to_core(slot, tt, j, k):
            remote(
                og_piece(slot, tt, j), og_piece(slot, tt, j),
                ogc_send.at[k], og_sem.at[slot, j, tt], at_t(tx * 2 + 1 - core),
            )

        def stage_a(i):
            j = mirrored(nz - 1 - i)

            def one(slot):
                arrived(og_piece(slot, t, j), og_sem.at[slot, j, t])
                for k in range(1, nx):
                    remote(
                        og_piece(slot, t, j), og_piece(slot, t, j),
                        ogx_send.at[k - 1], og_sem.at[slot, j, t],
                        at_t(lax.rem(tx + k, nx) * 2 + core),
                    )
                to_core(slot, t, j, 0)

            each_slot(one)

        def stage_b(i):
            j = mirrored(nz - 1 - i)

            def one(slot):
                for k in range(1, nx):
                    tt = lax.rem(tx + k, nx) * 2 + core
                    arrived(og_piece(slot, tt, j), og_sem.at[slot, j, tt])
                    to_core(slot, tt, j, k)

            each_slot(one)

        def stage_c(i):
            j = mirrored(nz - 1 - i)

            def one(slot):
                for k in range(nx):
                    tt = k * 2 + 1 - core
                    arrived(og_piece(slot, tt, j), og_sem.at[slot, j, tt])

            each_slot(one)
            for slot in range(slots if half == 2 else 0):
                for r in range(ny):
                    og_t[j, r * rows : (r + 1) * rows, slot * tokens : (slot + 1) * tokens] = (
                        ograw[slot, :, block(j * ny + r, rows)].T
                    )

        def partial(j, c):
            if half > 2:
                total = None
                for slot in range(slots):
                    term = lax.dot_general(
                        ograw[slot, :, rows_of(j)], h[c, slot * tokens : (slot + 1) * tokens],
                        (((0,), (0,)), ((), ())), preferred_element_type=F32,
                    )
                    total = term if total is None else total + term
                return total
            return jnp.dot(og_t[j], h[c], preferred_element_type=F32)

        def took(idx, c):
            arrived(recv.at[idx, c], recv_sem.at[idx, c])

        steps = n + (nz - 3) * lag + fin_lag

        def step(s, carry):
            f = s - (inner_z - 1) * lag
            f_on = jnp.logical_and(f >= 0, f < n)

            @pl.when(s == 0)
            def _():
                stage_a(0)

            def far(jm):
                j = mirrored(jm)

                def go():
                    own = partial(j, f)
                    if half == 2:
                        send[j, f] = own.astype(BF16)
                    else:
                        @pl.when(zm == 1)
                        def _():
                            send[j, f] = own.astype(BF16)

                        @pl.when(zm > 1)
                        def _():
                            took(far_slot(j), f)
                            send[j, f] = (own + recv[far_slot(j), f].astype(F32)).astype(BF16)

                    remote(
                        send.at[j, f], recv.at[far_slot(j), f],
                        s_send.at[j], recv_sem.at[far_slot(j), f], at(z + toward, y),
                    )

                if jm >= half:
                    pl.when(f_on)(go)
                else:
                    pl.when(jnp.logical_and(f_on, jm > zm))(go)

            for i in range(nz - 2):
                @pl.when(s == 0)
                def _():
                    stage_a(i + 1)
                    stage_b(i)
                    stage_c(i)

                if i == 0:
                    @pl.when(f_on)
                    def _():
                        arrived(h.at[f, block(y, tokens)], h_sem.at[y, f])
                        each_slot(lambda slot: arrived(h.at[f, block(slot, tokens)], h_sem.at[slot, f]))

                        @pl.when(f + ahead < n)
                        def _():
                            y_send(f + ahead)

                far(nz - 1 - i)

            @pl.when(s == 1)
            def _():
                stage_a(nz - 1)
                for i in range(nz - 2, nz):
                    stage_b(i)
                    stage_c(i)

            c = s - (nz - 2 - inner_z) * lag

            @pl.when(jnp.logical_and(c >= 0, c < n))
            def _():
                def near(jm):
                    j = mirrored(jm)
                    own = partial(j, c)
                    took(near_slot(j), c)
                    send[j, c] = (own + recv[near_slot(j), c].astype(F32)).astype(BF16)

                    def to_end():
                        for k in range(ny):
                            p = lax.rem(y + 1 + k, ny)
                            remote(
                                send.at[j, c, block(p, rows)], fin.at[y, c],
                                s_send.at[j], fin_sem.at[y, c], at(z_end, p),
                            )

                    def onward():
                        remote(
                            send.at[j, c], recv.at[near_slot(j), c],
                            s_send.at[j], recv_sem.at[near_slot(j), c], at(z - toward, y),
                        )

                    if jm > 0:
                        onward()
                    else:
                        when(near_end, to_end)
                        if half > 2:
                            pl.when(zm > 1)(onward)

                for jm in range(half - 1):
                    if jm == 0:
                        near(jm)
                    else:
                        pl.when(jm < zm)(functools.partial(near, jm))

                acc[...] = partial(z, c)
                took(near_slot(z), c)
                acc[...] += recv[near_slot(z), c].astype(F32)
                if half > 2:
                    @pl.when(zm > 1)
                    def _():
                        took(far_slot(z), c)
                        acc[...] += recv[far_slot(z), c].astype(F32)

                for k in range(1, ny):
                    p = lax.rem(y + k, ny)
                    send[z, c, block(p, rows)] = acc[block(p, rows)].astype(BF16)
                    remote(
                        send.at[z, c, block(p, rows)], fin.at[y, c],
                        s_send.at[z], fin_sem.at[y, c], at_y(k),
                    )
                process(y * n + c, acc[block(y, rows)])

            g = c - fin_lag

            @pl.when(jnp.logical_and(g >= 0, g < n))
            def _():
                for k in range(1, ny):
                    process_fin(lax.rem(y + k, ny), g)

            return carry

        lax.fori_loop(0, steps, step, 0)

    g_all[t, :rows] = gram[...]
    total = jnp.sum(jnp.sum(norm[...], axis=0, keepdims=True), axis=1, keepdims=True)
    g_all[t, rows:] = jnp.broadcast_to(total, (8, rows))
    for k in range(1, nt):
        pltpu.make_async_remote_copy(
            g_all.at[t], g_all.at[t], g_send.at[k - 1], g_recv.at[t],
            device_id=at_t(lax.rem(t + k, nt)), device_id_type=MESH,
        ).start()
    for k in range(nt):
        @pl.when(k != t)
        def _():
            pltpu.make_async_copy(g_all.at[k], g_all.at[k], g_recv.at[k]).wait()
    summed = g_all[0]
    for k in range(1, nt):
        summed = summed + g_all[k]
    inverse = 1.0 / (jnp.sqrt(summed[rows : rows + 1]) + 1e-07)
    current = summed[:rows] * inverse * inverse
    eye = (
        lax.broadcasted_iota(jnp.int32, (rows, rows), 0)
        == lax.broadcasted_iota(jnp.int32, (rows, rows), 1)
    ).astype(F32)
    map_all = None
    for iteration in range(ITERS):
        square = exact_dot(current, current)
        map_one = quintic_a * eye + quintic_b * current + quintic_c * square
        map_all = map_one if map_all is None else exact_dot(map_one, map_all)
        mapped = exact_dot(map_one, current)
        if iteration < ITERS - 1:
            current = exact_dot(mapped, map_one)
    energy = jnp.sum(mapped * map_one, axis=0, keepdims=True)
    second_out = beta_two * sec_ref[...] + (1.0 - beta_two) * energy
    secout_ref[...] = second_out
    scale = jnp.sqrt(ff / second_out) * inverse
    final = jnp.sum(eye * scale, axis=1, keepdims=True) * map_all
    final_ref[...] = final

    def sent(ref, sem):
        pltpu.make_async_copy(ref, ref, sem).wait()

    blocks = h.at[:, pl.ds(0, tokens)]
    og_piece_all = ograw.at[0, pl.ds(0, tau)]
    for k in range(1, ny):
        sent(blocks, hy_send.at[k - 1])
        sent(og_piece_all, og_send.at[k])

    @pl.when(is_end)
    def _():
        sent(og_piece_all, og_send.at[0])
        sent(blocks, end_send)
        for k in range(1, ny):
            sent(blocks, fwd_send.at[k - 1])

    @pl.when(jnp.logical_not(is_end))
    def _():
        def og_gather(count):
            pieces = ograw.at[pl.ds(0, count), pl.ds(0, tau)]
            for k in range(1, nx):
                sent(pieces, ogx_send.at[k - 1])
            for k in range(nx):
                sent(pieces, ogc_send.at[k])

        if half == 2:
            og_gather(slots - 1)
        else:
            pl.when(zm == 1)(functools.partial(og_gather, slots - 1))
            pl.when(zm > 1)(functools.partial(og_gather, ny - 1))
        for j in range(nz):
            @pl.when(z != j)
            def _():
                sent(send.at[j], s_send.at[j])

        if ny > 1:
            own = send.at[z, :, pl.ds(0, (ny - 1) * rows)]
            sent(own, s_send.at[z])

    for k in range(1, nt):
        sent(g_all.at[0], g_send.at[k - 1])


def write_kernel(n_chunks, x, mom, final_ref, sec_ref, upd_hbm, momout_hbm, secout_ref, out, mom_sem, upd_sem):
    width = x.shape[2]

    def columns(c):
        return pl.ds(pl.multiple_of(c * width, width), width)

    high = final_ref[...].astype(BF16)
    low = (final_ref[...] - high.astype(F32)).astype(BF16)
    secout_ref[...] = sec_ref[...]

    def finish(c, carry):
        pltpu.make_async_copy(mom.at[c], momout_hbm.at[:, columns(c)], mom_sem).start()
        panel = x[c]
        result = jnp.dot(high, panel, preferred_element_type=F32)
        result += jnp.dot(low, panel, preferred_element_type=F32)
        out[c] = result.astype(BF16)
        pltpu.make_async_copy(out.at[c], upd_hbm.at[:, columns(c)], upd_sem).start()
        return carry

    lax.fori_loop(0, n_chunks, finish, 0)
    pltpu.make_async_copy(mom, mom, mom_sem).wait()
    pltpu.make_async_copy(out, out, upd_sem).wait()


def body(nz, ny, nt, out_grad, hidden, momentum, second):
    tokens, cols = hidden.shape
    rows = momentum.shape[0]
    part = cols // ny
    width = 128
    n = part // width
    group = ny * rows
    dma = pltpu.SemaphoreType.DMA
    anywhere = pl.BlockSpec(memory_space=pltpu.HBM)
    vmem = pl.BlockSpec(memory_space=pltpu.VMEM)
    panel, mom, final, second_out = pl.pallas_call(
        functools.partial(kernel, nz, ny, nt, n, float(cols * nt)),
        out_shape=(
            jax.ShapeDtypeStruct((ny * n, rows, width), BF16),
            jax.ShapeDtypeStruct((ny * n, rows, width), F32),
            jax.ShapeDtypeStruct((rows, rows), F32),
            jax.ShapeDtypeStruct((1, rows), F32),
        ),
        in_specs=[anywhere, anywhere, anywhere, vmem],
        out_specs=(vmem, vmem, vmem, vmem),
        scratch_shapes=[
            pltpu.VMEM((n, 2 * ny * tokens, width), BF16),
            pltpu.VMEM((2 * ny, tokens, nz * group), BF16),
            pltpu.VMEM((nz if nz == 4 else 1, group, 2 * ny * tokens), BF16),
            pltpu.VMEM((nz + 1, n, group, width), BF16),
            pltpu.VMEM((nz, n, group, width), BF16),
            pltpu.VMEM((ny, n, rows, width), BF16),
            pltpu.VMEM((group, width), F32),
            pltpu.VMEM((rows, rows), F32),
            pltpu.VMEM((rows, width), F32),
            pltpu.VMEM((nt, rows + 8, rows), F32),
            dma((2 * ny, n)),
            dma((2 * ny, nz, nt)),
            dma,
            dma((nz + 1, n)),
            dma((ny, n)),
            dma,
            dma((max(ny - 1, 1),)),
            dma,
            dma((max(ny - 1, 1),)),
            dma((ny,)),
            dma((max(nt // 2 - 1, 1),)),
            dma((nt // 2,)),
            dma((nz,)),
            dma((max(nt - 1, 1),)),
            dma((nt,)),
        ],
        compiler_params=pltpu.CompilerParams(
            collective_id=0, has_side_effects=True, vmem_limit_bytes=59 * 1024 * 1024
        ),
        name="normuon",
    )(out_grad, hidden, momentum, second.reshape(1, rows))
    update, momentum_out, second_out = pl.pallas_call(
        functools.partial(write_kernel, ny * n),
        out_shape=(
            jax.ShapeDtypeStruct((rows, cols), BF16),
            jax.ShapeDtypeStruct((rows, cols), F32),
            jax.ShapeDtypeStruct((1, rows), F32),
        ),
        in_specs=[vmem] * 4,
        out_specs=(anywhere, anywhere, vmem),
        scratch_shapes=[pltpu.VMEM((ny * n, rows, width), BF16), dma, dma],
        compiler_params=pltpu.CompilerParams(vmem_limit_bytes=16 * 1024 * 1024),
        name="write_results",
    )(panel, mom, final, second_out)
    return update, momentum_out, second_out.reshape(rows)


def solution(mesh):
    nz, ny = line_split(mesh.shape["dp"])
    placed = (P("dp", None), P("dp", "tensor"), P("dp", "tensor"), P("dp"))
    return jax.shard_map(
        functools.partial(body, nz, ny, mesh.shape["tensor"]),
        mesh=mesh,
        in_specs=placed,
        out_specs=(P("dp", "tensor"), P("dp", "tensor"), P("dp")),
        check_vma=False,
    )
```

time: 155 us -> 133 us (0.86)
  Pallas kernels: 152 us -> 126 us
  local copies, waits for them, and re-layouts: 1.69 us -> 5.04 us
    pallas_call x2, Pallas kernels: 152 us -> 126 us  [the longest x1 117 us: body(): pl.pallas_call(functools.partial(kernel, nz, ny, nt, n, float(cols * nt))...]
    unnamed x4 -> x8, local copies, waits for them, and re-layouts: 1.69 us -> 5.04 us
where the time goes in v1:
time: 133 us; the launch traced here: 132 us
  Pallas kernels  126 us (95%)
  local copies, waits for them, and re-layouts  5.04 us (4%)
    pallas_call x1, Pallas kernels, body(): pl.pallas_call(functools.partial(kernel, nz, ny, nt, n, float(cols * nt))...  117 us
    pallas_call x1, Pallas kernels, body(): pl.pallas_call(functools.partial(write_kernel, ny * n), out_shape=(jax.Sh...  9.64 us
    unnamed x8, local copies, waits for them, and re-layouts  5.04 us

profile of v1, /device:TPU:0, one launch (start us, length us, event | category | flops | bytes accessed | tf_op | source)
XLA Modules:
  0.0 132.2 jit_solution(1158304764753206791)
XLA Ops:
  0.6 116.8 %normuon.1 = (bf16[56,128,128]{2,1,0:T(8,128)(2,1)}, f32[56,128,128]{2,1,0:T(8,128)}, f32[128,128]{1,0:T(8,128)}, f32[1,128]{1,0:T(1,128)}) custom-call(bf16[256,1024]{1,0:T(8,128)(2,1)} %og_hbm.1, bf16[256,7168]{1,0:T(8,128)(2,1)} %h_hbm.1, f32[128,7168]{1,0:T(8,128)} %mom_hbm.1, f32[1,128]{1,0:T(1,128)} %bitcast.2), custom_call_target="tpu_custom_call" | custom-call | tf_op jit(solution)/shard_map/normuon/pallas_call | solution.py:582
  117.5 0.0 copy-start
  117.5 2.0 %copy-done = f32[56,128,128]{2,1,0:T(8,128)S(1)} copy-done((f32[56,128,128]{2,1,0:T(8,128)S(1)}, f32[56,128,128]{2,1,0:T(8,128)}, u32[]{:S(2)}) %copy-start) | copy-done | bytes 3670040
  119.5 0.0 copy-start.1
  119.5 1.5 %copy-done.1 = bf16[56,128,128]{2,1,0:T(8,128)(2,1)S(1)} copy-done((bf16[56,128,128]{2,1,0:T(8,128)(2,1)S(1)}, bf16[56,128,128]{2,1,0:T(8,128)(2,1)}, u32[]{:S(2)}) %copy-start.1) | copy-done | bytes 1835032
  121.0 0.0 copy-start.2
  121.0 0.8 copy-done.2
  121.9 0.0 copy-start.3
  121.9 0.7 copy-done.3
  122.5 9.6 %write_results.1 = (bf16[128,7168]{1,0:T(8,128)(2,1)}, f32[128,7168]{1,0:T(8,128)}, f32[1,128]{1,0:T(1,128)}) custom-call(bf16[56,128,128]{2,1,0:T(8,128)(2,1)S(1)} %copy-done.1, f32[56,128,128]{2,1,0:T(8,128)S(1)} %copy-done, f32[128,128]{1,0:T(8,128)S(1)} %copy-done.2, f32[1,128]{1,0:T(1,128)S(1)} %copy-done.3), custom_call_target="tpu_custom_call" | custom-call | tf_op jit(solution)/shard_map/write_results/pallas_call | solution.py:624
Async XLA Ops:
  117.5 2.0 %copy-start = (f32[56,128,128]{2,1,0:T(8,128)S(1)}, f32[56,128,128]{2,1,0:T(8,128)}, u32[]{:S(2)}) copy-start(f32[56,128,128]{2,1,0:T(8,128)} %get-tuple-element.11.mom) | copy-start | bytes 11010052
  119.5 1.5 %copy-start.1 = (bf16[56,128,128]{2,1,0:T(8,128)(2,1)S(1)}, bf16[56,128,128]{2,1,0:T(8,128)(2,1)}, u32[]{:S(2)}) copy-start(bf16[56,128,128]{2,1,0:T(8,128)(2,1)} %get-tuple-element.10.x) | copy-start | bytes 5505028
  121.0 0.8 copy-start.2
  121.9 0.7 copy-start.3

commit v2 on v1

--- a/solution.py
+++ b/solution.py
@@ -32,20 +32,20 @@
 
 def kernel(
     nz, ny, nt, n, ff,
-    og_hbm, h_hbm, mom_hbm, sec_ref,
+    og_hbm, h_hbm, mom_hbm, sec_hbm,
     x, mom, final_ref, secout_ref,
-    h, ograw, og_t, recv, send, fin, acc, gram, norm, g_all,
-    h_sem, og_sem, og_own, recv_sem, fin_sem, mom_sem,
+    h, ograw, og_t, recv, send, fin, acc, gram, g_all, sec_ref,
+    h_sem, og_sem, og_own, recv_sem, fin_sem, mom_sem, sec_sem,
     hy_send, end_send, fwd_send, og_send, ogx_send, ogc_send, s_send, g_send, g_recv,
 ):
     tokens, part = h_hbm.shape[0], h_hbm.shape[1] // ny
-    rows, width = x.shape[1], x.shape[2]
+    rows, width = x.shape[0], part // n
     group = ny * rows
     tau = tokens // nt
     nx = nt // 2
     slots = 2 * ny
     half = nz // 2
-    ahead, end_ahead, lag, fin_lag = 6, 3, 2, 2
+    ahead, end_ahead, lag, fin_lag = 6, 1, 2, 2
     d = lax.axis_index("dp")
     t = lax.axis_index("tensor")
     z, y = d // ny, lax.rem(d, ny)
@@ -135,7 +135,10 @@
         greeted + jnp.where(zm == 0, ny, 0) + jnp.where(zm == 1, ny + 1, 0) + jnp.where(zm > 1, 2, 0),
     )
 
-    piece = block(t, tau)
+    def share(i, tt):
+        if i == 0:
+            return block(lax.rem(tt, 2), tokens // 2)
+        return block(tt, tau)
 
     def rows_of(j):
         return block(j, group)
@@ -148,17 +151,16 @@
                 hy_send.at[k - 1], h_sem.at[y, c], at_y(k),
             )
 
-    def mom_load(c, carry):
-        pltpu.make_async_copy(mom_hbm.at[:, block(c, width)], mom.at[c], mom_sem).start()
-        return carry
+    def mom_load():
+        pltpu.make_async_copy(mom_hbm, mom, mom_sem).start()
+        pltpu.make_async_copy(sec_hbm, sec_ref, sec_sem).start()
 
     def process(q, grad):
-        momentum_out = beta_one * mom[q] + grad
-        nesterov = grad + beta_one * momentum_out
-        mom[q] = momentum_out
-        panel = nesterov.astype(BF16)
-        x[q] = panel
-        norm[...] += nesterov * nesterov
+        cols = block(q, width)
+        momentum_out = beta_one * mom[:, cols] + grad
+        mom[:, cols] = momentum_out
+        panel = (grad + beta_one * momentum_out).astype(BF16)
+        x[:, cols] = panel
         gram[...] += lax.dot_general(
             panel, panel, (((1,), (1,)), ((), ())), preferred_element_type=F32
         )
@@ -175,8 +177,8 @@
             j = mirrored(nz - 1 - i)
             for k in range(ny):
                 remote(
-                    og_hbm.at[piece, rows_of(j)], ograw.at[ny + y, piece, rows_of(j)],
-                    og_send.at[k], og_sem.at[ny + y, j, t], at(z_in, lax.rem(y + k, ny)),
+                    og_hbm.at[share(i, t), rows_of(j)], ograw.at[ny + y, share(i, t), rows_of(j)],
+                    og_send.at[min(i, 1), k], og_sem.at[ny + y, j, t], at(z_in, lax.rem(y + k, ny)),
                 )
 
         def own_to_inner(c):
@@ -200,9 +202,8 @@
             return carry
 
         lax.fori_loop(min(2, n), n, rest, 0)
-        lax.fori_loop(0, ny * n, mom_load, 0)
+        mom_load()
         gram[...] = jnp.zeros_like(gram)
-        norm[...] = jnp.zeros_like(norm)
 
         def forward(c, carry):
             for k in range(1, ny):
@@ -220,7 +221,8 @@
             return carry
 
         lax.fori_loop(0, n, forward, 0)
-        pltpu.make_async_copy(mom, mom, mom_sem).wait()
+        pltpu.make_async_copy(mom_hbm, mom, mom_sem).wait()
+        pltpu.make_async_copy(sec_hbm, sec_ref, sec_sem).wait()
 
         def finish(c, carry):
             for k in range(ny):
@@ -236,8 +238,8 @@
             j = mirrored(nz - 1 - i)
             for k in range(1, ny):
                 remote(
-                    og_hbm.at[piece, rows_of(j)], ograw.at[y, piece, rows_of(j)],
-                    og_send.at[k], og_sem.at[y, j, t], at_y(k),
+                    og_hbm.at[share(i, t), rows_of(j)], ograw.at[y, share(i, t), rows_of(j)],
+                    og_send.at[min(i, 1), k], og_sem.at[y, j, t], at_y(k),
                 )
         for c in range(min(ahead, n)):
             y_send(c)
@@ -250,16 +252,16 @@
             return carry
 
         lax.fori_loop(0, n, own_load, 0)
-        lax.fori_loop(0, ny * n, mom_load, 0)
+        mom_load()
         gram[...] = jnp.zeros_like(gram)
-        norm[...] = jnp.zeros_like(norm)
         if half > 2:
             @pl.when(zm > 1)
             def _():
                 h[:, ny * tokens :] = jnp.zeros((n, ny * tokens, width), BF16)
                 ograw[ny:] = jnp.zeros((ny,) + ograw.shape[1:], BF16)
 
-        pltpu.make_async_copy(mom, mom, mom_sem).wait()
+        pltpu.make_async_copy(mom_hbm, mom, mom_sem).wait()
+        pltpu.make_async_copy(sec_hbm, sec_ref, sec_sem).wait()
         pltpu.make_async_copy(og_hbm, ograw.at[y], og_own).wait()
 
         def each_slot(fn):
@@ -272,48 +274,51 @@
 
             when(near_end, from_end)
 
-        def og_piece(slot, tt, j):
-            return ograw.at[slot, block(tt, tau), rows_of(j)]
-
-        def to_core(slot, tt, j, k):
+        def og_piece(i, slot, tt):
+            return ograw.at[slot, share(i, tt), rows_of(mirrored(nz - 1 - i))]
+
+        def to_core(i, slot, tt, k):
             remote(
-                og_piece(slot, tt, j), og_piece(slot, tt, j),
-                ogc_send.at[k], og_sem.at[slot, j, tt], at_t(tx * 2 + 1 - core),
+                og_piece(i, slot, tt), og_piece(i, slot, tt), ogc_send.at[min(i, 1), k],
+                og_sem.at[slot, mirrored(nz - 1 - i), tt], at_t(tx * 2 + 1 - core),
             )
 
+        def og_took(i, slot, tt):
+            arrived(og_piece(i, slot, tt), og_sem.at[slot, mirrored(nz - 1 - i), tt])
+
         def stage_a(i):
-            j = mirrored(nz - 1 - i)
-
             def one(slot):
-                arrived(og_piece(slot, t, j), og_sem.at[slot, j, t])
-                for k in range(1, nx):
-                    remote(
-                        og_piece(slot, t, j), og_piece(slot, t, j),
-                        ogx_send.at[k - 1], og_sem.at[slot, j, t],
-                        at_t(lax.rem(tx + k, nx) * 2 + core),
-                    )
-                to_core(slot, t, j, 0)
+                og_took(i, slot, t)
+                if i > 0:
+                    for k in range(1, nx):
+                        remote(
+                            og_piece(i, slot, t), og_piece(i, slot, t), ogx_send.at[k - 1],
+                            og_sem.at[slot, mirrored(nz - 1 - i), t],
+                            at_t(lax.rem(tx + k, nx) * 2 + core),
+                        )
+                to_core(i, slot, t, 0)
 
             each_slot(one)
 
         def stage_b(i):
-            j = mirrored(nz - 1 - i)
-
             def one(slot):
                 for k in range(1, nx):
                     tt = lax.rem(tx + k, nx) * 2 + core
-                    arrived(og_piece(slot, tt, j), og_sem.at[slot, j, tt])
-                    to_core(slot, tt, j, k)
-
-            each_slot(one)
+                    og_took(i, slot, tt)
+                    to_core(i, slot, tt, k)
+
+            if i > 0:
+                each_slot(one)
 
         def stage_c(i):
             j = mirrored(nz - 1 - i)
 
             def one(slot):
-                for k in range(nx):
-                    tt = k * 2 + 1 - core
-                    arrived(og_piece(slot, tt, j), og_sem.at[slot, j, tt])
+                if i == 0:
+                    og_took(i, slot, tx * 2 + 1 - core)
+                else:
+                    for k in range(nx):
+                        og_took(i, slot, k * 2 + 1 - core)
 
             each_slot(one)
             for slot in range(slots if half == 2 else 0):
@@ -466,9 +471,7 @@
 
         lax.fori_loop(0, steps, step, 0)
 
-    g_all[t, :rows] = gram[...]
-    total = jnp.sum(jnp.sum(norm[...], axis=0, keepdims=True), axis=1, keepdims=True)
-    g_all[t, rows:] = jnp.broadcast_to(total, (8, rows))
+    g_all[t] = gram[...].astype(BF16)
     for k in range(1, nt):
         pltpu.make_async_remote_copy(
             g_all.at[t], g_all.at[t], g_send.at[k - 1], g_recv.at[t],
@@ -478,15 +481,16 @@
         @pl.when(k != t)
         def _():
             pltpu.make_async_copy(g_all.at[k], g_all.at[k], g_recv.at[k]).wait()
-    summed = g_all[0]
+    summed = g_all[0].astype(F32)
     for k in range(1, nt):
-        summed = summed + g_all[k]
-    inverse = 1.0 / (jnp.sqrt(summed[rows : rows + 1]) + 1e-07)
-    current = summed[:rows] * inverse * inverse
+        summed = summed + g_all[k].astype(F32)
     eye = (
         lax.broadcasted_iota(jnp.int32, (rows, rows), 0)
         == lax.broadcasted_iota(jnp.int32, (rows, rows), 1)
     ).astype(F32)
+    total = jnp.sum(jnp.sum(summed * eye, axis=0, keepdims=True), axis=1, keepdims=True)
+    inverse = 1.0 / (jnp.sqrt(total) + 1e-07)
+    current = summed * inverse * inverse
     map_all = None
     for iteration in range(ITERS):
         square = exact_dot(current, current)
@@ -506,14 +510,18 @@
         pltpu.make_async_copy(ref, ref, sem).wait()
 
     blocks = h.at[:, pl.ds(0, tokens)]
-    og_piece_all = ograw.at[0, pl.ds(0, tau)]
+
+    def og_sent(k):
+        sent(ograw.at[0, pl.ds(0, tokens // 2), pl.ds(0, group)], og_send.at[0, k])
+        sent(ograw.at[0, pl.ds(0, tau), pl.ds(0, (nz - 1) * group)], og_send.at[1, k])
+
     for k in range(1, ny):
         sent(blocks, hy_send.at[k - 1])
-        sent(og_piece_all, og_send.at[k])
+        og_sent(k)
 
     @pl.when(is_end)
     def _():
-        sent(og_piece_all, og_send.at[0])
+        og_sent(0)
         sent(blocks, end_send)
         for k in range(1, ny):
             sent(blocks, fwd_send.at[k - 1])
@@ -521,11 +529,12 @@
     @pl.when(jnp.logical_not(is_end))
     def _():
         def og_gather(count):
-            pieces = ograw.at[pl.ds(0, count), pl.ds(0, tau)]
+            pieces = ograw.at[pl.ds(0, count), pl.ds(0, tau), pl.ds(0, (nz - 1) * group)]
+            sent(ograw.at[pl.ds(0, count), pl.ds(0, tokens // 2), pl.ds(0, group)], ogc_send.at[0, 0])
             for k in range(1, nx):
                 sent(pieces, ogx_send.at[k - 1])
             for k in range(nx):
-                sent(pieces, ogc_send.at[k])
+                sent(pieces, ogc_send.at[1, k])
 
         if half == 2:
             og_gather(slots - 1)
@@ -545,28 +554,23 @@
         sent(g_all.at[0], g_send.at[k - 1])
 
 
-def write_kernel(n_chunks, x, mom, final_ref, sec_ref, upd_hbm, momout_hbm, secout_ref, out, mom_sem, upd_sem):
-    width = x.shape[2]
-
-    def columns(c):
-        return pl.ds(pl.multiple_of(c * width, width), width)
-
+def write_kernel(x, mom, final_ref, sec_ref, upd_hbm, momout_hbm, secout_ref, out, mom_sem, upd_sem):
+    pltpu.make_async_copy(mom, momout_hbm, mom_sem).start()
     high = final_ref[...].astype(BF16)
-    low = (final_ref[...] - high.astype(F32)).astype(BF16)
     secout_ref[...] = sec_ref[...]
+    cols = x.shape[1]
+    width = 512 if cols % 512 == 0 else 128
+    n = cols // width
 
     def finish(c, carry):
-        pltpu.make_async_copy(mom.at[c], momout_hbm.at[:, columns(c)], mom_sem).start()
-        panel = x[c]
-        result = jnp.dot(high, panel, preferred_element_type=F32)
-        result += jnp.dot(low, panel, preferred_element_type=F32)
-        out[c] = result.astype(BF16)
-        pltpu.make_async_copy(out.at[c], upd_hbm.at[:, columns(c)], upd_sem).start()
+        part = pl.ds(pl.multiple_of(c * width, width), width)
+        out[:, part] = jnp.dot(high, x[:, part], preferred_element_type=F32).astype(BF16)
+        pltpu.make_async_copy(out.at[:, part], upd_hbm.at[:, part], upd_sem.at[0]).start()
         return carry
 
-    lax.fori_loop(0, n_chunks, finish, 0)
-    pltpu.make_async_copy(mom, mom, mom_sem).wait()
-    pltpu.make_async_copy(out, out, upd_sem).wait()
+    lax.fori_loop(0, n, finish, 0)
+    pltpu.make_async_copy(mom, momout_hbm, mom_sem).wait()
+    pltpu.make_async_copy(out, upd_hbm, upd_sem.at[0]).wait()
 
 
 def body(nz, ny, nt, out_grad, hidden, momentum, second):
@@ -582,12 +586,12 @@
     panel, mom, final, second_out = pl.pallas_call(
         functools.partial(kernel, nz, ny, nt, n, float(cols * nt)),
         out_shape=(
-            jax.ShapeDtypeStruct((ny * n, rows, width), BF16),
-            jax.ShapeDtypeStruct((ny * n, rows, width), F32),
+            jax.ShapeDtypeStruct((rows, cols), BF16),
+            jax.ShapeDtypeStruct((rows, cols), F32),
             jax.ShapeDtypeStruct((rows, rows), F32),
             jax.ShapeDtypeStruct((1, rows), F32),
         ),
-        in_specs=[anywhere, anywhere, anywhere, vmem],
+        in_specs=[anywhere] * 4,
         out_specs=(vmem, vmem, vmem, vmem),
         scratch_shapes=[
             pltpu.VMEM((n, 2 * ny * tokens, width), BF16),
@@ -598,31 +602,37 @@
             pltpu.VMEM((ny, n, rows, width), BF16),
             pltpu.VMEM((group, width), F32),
             pltpu.VMEM((rows, rows), F32),
-            pltpu.VMEM((rows, width), F32),
-            pltpu.VMEM((nt, rows + 8, rows), F32),
+            pltpu.VMEM((nt, rows, rows), BF16),
+            pltpu.VMEM((1, rows), F32),
             dma((2 * ny, n)),
             dma((2 * ny, nz, nt)),
             dma,
             dma((nz + 1, n)),
             dma((ny, n)),
             dma,
+            dma,
             dma((max(ny - 1, 1),)),
             dma,
             dma((max(ny - 1, 1),)),
-            dma((ny,)),
+            dma((2, ny)),
             dma((max(nt // 2 - 1, 1),)),
-            dma((nt // 2,)),
+            dma((2, nt // 2)),
             dma((nz,)),
             dma((max(nt - 1, 1),)),
             dma((nt,)),
         ],
         compiler_params=pltpu.CompilerParams(
-            collective_id=0, has_side_effects=True, vmem_limit_bytes=59 * 1024 * 1024
+            collective_id=0, has_side_effects=True, vmem_limit_bytes=48 * 1024 * 1024
         ),
         name="normuon",
-    )(out_grad, hidden, momentum, second.reshape(1, rows))
+    )(
+        *(
+            pltpu.with_memory_space_constraint(v, pltpu.HBM)
+            for v in (out_grad, hidden, momentum, second.reshape(1, rows))
+        )
+    )
     update, momentum_out, second_out = pl.pallas_call(
-        functools.partial(write_kernel, ny * n),
+        write_kernel,
         out_shape=(
             jax.ShapeDtypeStruct((rows, cols), BF16),
             jax.ShapeDtypeStruct((rows, cols), F32),
@@ -630,7 +640,7 @@
         ),
         in_specs=[vmem] * 4,
         out_specs=(anywhere, anywhere, vmem),
-        scratch_shapes=[pltpu.VMEM((ny * n, rows, width), BF16), dma, dma],
+        scratch_shapes=[pltpu.VMEM((rows, cols), BF16), dma, dma((2,))],
         compiler_params=pltpu.CompilerParams(vmem_limit_bytes=16 * 1024 * 1024),
         name="write_results",
     )(panel, mom, final, second_out)

time: 133 us -> 116 us (0.87)
  Pallas kernels: 126 us -> 115 us
  local copies, waits for them, and re-layouts: 5.04 us -> 0 us
    pallas_call x1, Pallas kernels: 9.64 us -> 3.67 us  [body(): pl.pallas_call(write_kernel, out_shape=(jax.ShapeDtypeStruct((rows, cols)...]
    pallas_call x1, Pallas kernels: 117 us -> 112 us  [body(): pl.pallas_call(functools.partial(kernel, nz, ny, nt, n, float(cols * nt))...]
    unnamed x8 -> x0, local copies, waits for them, and re-layouts: 5.04 us -> none
where the time goes in v2:
time: 116 us
  Pallas kernels  115 us (99%)
    pallas_call x1, Pallas kernels, body(): pl.pallas_call(functools.partial(kernel, nz, ny, nt, n, float(cols * nt))...  112 us
    pallas_call x1, Pallas kernels, body(): pl.pallas_call(write_kernel, out_shape=(jax.ShapeDtypeStruct((rows, cols)...  3.67 us

profile of v2, /device:TPU:0, one launch (start us, length us, event | category | flops | bytes accessed | tf_op | source)
XLA Modules:
  0.0 116.0 jit_solution(11318969432354116529)
XLA Ops:
  0.6 111.6 %normuon.1 = (bf16[128,7168]{1,0:T(8,128)(2,1)S(1)}, f32[128,7168]{1,0:T(8,128)S(1)}, f32[128,128]{1,0:T(8,128)S(1)}, f32[1,128]{1,0:T(1,128)S(1)}) custom-call(bf16[256,1024]{1,0:T(8,128)(2,1)} %og_hbm.1, bf16[256,7168]{1,0:T(8,128)(2,1)} %h_hbm.1, f32[128,7168]{1,0:T(8,128)} %mom_hbm.1, f32[1,128]{1,0:T(1,128)} %bitcast.2), custom_call_target="tpu_custom_call" | custom-call | tf_op jit(solution)/shard_map/normuon/pallas_call | solution.py:586
  112.3 3.7 %write_results.1 = (bf16[128,7168]{1,0:T(8,128)(2,1)}, f32[128,7168]{1,0:T(8,128)}, f32[1,128]{1,0:T(1,128)}) custom-call(bf16[128,7168]{1,0:T(8,128)(2,1)S(1)} %get-tuple-element.10.x, f32[128,7168]{1,0:T(8,128)S(1)} %get-tuple-element.11.mom, f32[128,128]{1,0:T(8,128)S(1)} %get-tuple-element.12.final_ref, f32[1,128]{1,0:T(1,128)S(1)} %get-tuple-element.13.sec_ref), custom_call_target="tpu_custom_call" | custom-call | tf_op jit(solution)/shard_map/write_results/pallas_call | solution.py:634

commit v3 on v2

--- a/solution.py
+++ b/solution.py
@@ -35,7 +35,7 @@
     og_hbm, h_hbm, mom_hbm, sec_hbm,
     x, mom, final_ref, secout_ref,
     h, ograw, og_t, recv, send, fin, acc, gram, g_all, sec_ref,
-    h_sem, og_sem, og_own, recv_sem, fin_sem, mom_sem, sec_sem,
+    h_sem, og_sem, og_own, ogy_send, recv_sem, fin_sem, mom_sem, sec_sem,
     hy_send, end_send, fwd_send, og_send, ogx_send, ogc_send, s_send, g_send, g_recv,
 ):
     tokens, part = h_hbm.shape[0], h_hbm.shape[1] // ny
@@ -45,7 +45,7 @@
     nx = nt // 2
     slots = 2 * ny
     half = nz // 2
-    ahead, end_ahead, lag, fin_lag = 6, 1, 2, 2
+    ahead, end_ahead, lag, late, fin_lag = nz + 1, 1, 2, 6, 2
     d = lax.axis_index("dp")
     t = lax.axis_index("tensor")
     z, y = d // ny, lax.rem(d, ny)
@@ -58,11 +58,13 @@
     def mirrored(jm):
         return jnp.where(lower, jm, nz - 1 - jm)
 
-    def far_slot(j):
-        return jnp.where(lower, j + 1, j)
-
-    def near_slot(j):
-        return jnp.where(lower, j, j + 1)
+    def far_slot(jm):
+        return half + jm
+
+    def onward_slot(jm):
+        if half == 2:
+            return nz - 1 - jm
+        return jnp.where(zm == half - 1, nz - 1 - jm, far_slot(jm))
 
     def at(zz, yy):
         return (zz * ny + yy, t)
@@ -148,7 +150,7 @@
             p = lax.rem(y + k, ny)
             remote(
                 h_hbm.at[:, columns(p, c)], h.at[c, block(y, tokens)],
-                hy_send.at[k - 1], h_sem.at[y, c], at_y(k),
+                hy_send.at[k - 1], h_sem.at[c], at_y(k),
             )
 
     def mom_load():
@@ -165,9 +167,11 @@
             panel, panel, (((1,), (1,)), ((), ())), preferred_element_type=F32
         )
 
-    def process_fin(p, c):
-        arrived(fin.at[p, c], fin_sem.at[p, c])
-        process(p * n + c, fin[p, c].astype(F32))
+    def process_fin(count, c):
+        arrived(fin.at[c, pl.ds(0, count)], fin_sem.at[c])
+        for k in range(ny - count, ny):
+            p = lax.rem(y + k, ny)
+            process(p * n + c, fin[c, p].astype(F32))
 
     @pl.when(is_end)
     def _():
@@ -175,26 +179,23 @@
 
         def og_to_inner(i):
             j = mirrored(nz - 1 - i)
-            for k in range(ny):
-                remote(
-                    og_hbm.at[share(i, t), rows_of(j)], ograw.at[ny + y, share(i, t), rows_of(j)],
-                    og_send.at[min(i, 1), k], og_sem.at[ny + y, j, t], at(z_in, lax.rem(y + k, ny)),
-                )
+            remote(
+                og_hbm.at[share(i, t), rows_of(j)], ograw.at[ny + y, share(i, t), rows_of(j)],
+                og_send.at[min(i, 1), 0], og_sem.at[ny + y, j, t], at(z_in, y),
+            )
 
         def own_to_inner(c):
             remote(
                 h_hbm.at[:, columns(y, c)], h.at[c, block(ny + y, tokens)],
-                end_send, h_sem.at[ny + y, c], at(z_in, y),
+                end_send, h_sem.at[c], at(z_in, y),
             )
 
         og_to_inner(0)
         for c in range(min(2, n)):
             y_send(c)
-        for i in range(1, nz):
+        for i in range(1, nz - 2):
             og_to_inner(i)
-            if i <= min(end_ahead, n):
-                own_to_inner(i - 1)
-        for c in range(min(nz - 1, end_ahead, n), min(end_ahead, n)):
+        for c in range(min(end_ahead, n)):
             own_to_inner(c)
 
         def rest(c, carry):
@@ -206,17 +207,22 @@
         gram[...] = jnp.zeros_like(gram)
 
         def forward(c, carry):
+            arrived(h.at[c, pl.ds(0, (ny - 1) * tokens)], h_sem.at[c])
             for k in range(1, ny):
                 p = lax.rem(y + k, ny)
-                arrived(h.at[c, block(p, tokens)], h_sem.at[p, c])
                 remote(
                     h.at[c, block(p, tokens)], h.at[c, block(ny + p, tokens)],
-                    fwd_send.at[k - 1], h_sem.at[ny + p, c], at(z_in, y),
+                    fwd_send.at[k - 1], h_sem.at[c], at(z_in, y),
                 )
 
             @pl.when(c + end_ahead < n)
             def _():
                 own_to_inner(c + end_ahead)
+
+            @pl.when(c == min(2, n) - 1)
+            def _():
+                for i in range(nz - 2, nz):
+                    og_to_inner(i)
 
             return carry
 
@@ -225,8 +231,7 @@
         pltpu.make_async_copy(sec_hbm, sec_ref, sec_sem).wait()
 
         def finish(c, carry):
-            for k in range(ny):
-                process_fin(lax.rem(y + k, ny), c)
+            process_fin(ny, c)
             return carry
 
         lax.fori_loop(0, n, finish, 0)
@@ -234,20 +239,23 @@
     @pl.when(jnp.logical_not(is_end))
     def _():
         near_end = inner_z == 1
-        for i in range(nz):
+        def og_to_peers(i):
             j = mirrored(nz - 1 - i)
             for k in range(1, ny):
                 remote(
                     og_hbm.at[share(i, t), rows_of(j)], ograw.at[y, share(i, t), rows_of(j)],
                     og_send.at[min(i, 1), k], og_sem.at[y, j, t], at_y(k),
                 )
-        for c in range(min(ahead, n)):
-            y_send(c)
+
+        og_to_peers(0)
+        y_send(0)
+        for i in range(1, nz - 2):
+            og_to_peers(i)
         pltpu.make_async_copy(og_hbm, ograw.at[y], og_own).start()
 
         def own_load(c, carry):
             pltpu.make_async_copy(
-                h_hbm.at[:, columns(y, c)], h.at[c, block(y, tokens)], h_sem.at[y, c]
+                h_hbm.at[:, columns(y, c)], h.at[c, block(y, tokens)], h_sem.at[c]
             ).start()
             return carry
 
@@ -260,19 +268,21 @@
                 h[:, ny * tokens :] = jnp.zeros((n, ny * tokens, width), BF16)
                 ograw[ny:] = jnp.zeros((ny,) + ograw.shape[1:], BF16)
 
-        pltpu.make_async_copy(mom_hbm, mom, mom_sem).wait()
-        pltpu.make_async_copy(sec_hbm, sec_ref, sec_sem).wait()
         pltpu.make_async_copy(og_hbm, ograw.at[y], og_own).wait()
 
-        def each_slot(fn):
+        def peer_slots(fn):
             for k in range(1, ny):
                 fn(lax.rem(y + k, ny))
 
             def from_end():
-                for p in range(ny):
-                    fn(ny + p)
+                for k in range(1, ny):
+                    fn(ny + lax.rem(y + k, ny))
 
             when(near_end, from_end)
+
+        def each_slot(fn):
+            peer_slots(fn)
+            when(near_end, functools.partial(fn, ny + y))
 
         def og_piece(i, slot, tt):
             return ograw.at[slot, share(i, tt), rows_of(mirrored(nz - 1 - i))]
@@ -286,19 +296,34 @@
         def og_took(i, slot, tt):
             arrived(og_piece(i, slot, tt), og_sem.at[slot, mirrored(nz - 1 - i), tt])
 
+        def share_out(i, slot):
+            if i > 0:
+                for k in range(1, nx):
+                    remote(
+                        og_piece(i, slot, t), og_piece(i, slot, t), ogx_send.at[k - 1],
+                        og_sem.at[slot, mirrored(nz - 1 - i), t],
+                        at_t(lax.rem(tx + k, nx) * 2 + core),
+                    )
+            to_core(i, slot, t, 0)
+
+        def stage_end(i):
+            def go():
+                og_took(i, ny + y, t)
+                for k in range(1, ny):
+                    remote(
+                        og_piece(i, ny + y, t), og_piece(i, ny + y, t), ogy_send.at[min(i, 1), k - 1],
+                        og_sem.at[ny + y, mirrored(nz - 1 - i), t], at_y(k),
+                    )
+                share_out(i, ny + y)
+
+            when(near_end, go)
+
         def stage_a(i):
             def one(slot):
                 og_took(i, slot, t)
-                if i > 0:
-                    for k in range(1, nx):
-                        remote(
-                            og_piece(i, slot, t), og_piece(i, slot, t), ogx_send.at[k - 1],
-                            og_sem.at[slot, mirrored(nz - 1 - i), t],
-                            at_t(lax.rem(tx + k, nx) * 2 + core),
-                        )
-                to_core(i, slot, t, 0)
-
-            each_slot(one)
+                share_out(i, slot)
+
+            peer_slots(one)
 
         def stage_b(i):
             def one(slot):
@@ -342,91 +367,130 @@
         def took(idx, c):
             arrived(recv.at[idx, c], recv_sem.at[idx, c])
 
-        steps = n + (nz - 3) * lag + fin_lag
+        steps = n + max((nz - 3) * lag, late) + fin_lag
 
         def step(s, carry):
-            f = s - (inner_z - 1) * lag
-            f_on = jnp.logical_and(f >= 0, f < n)
+            first = s - (inner_z - 1) * lag
 
             @pl.when(s == 0)
             def _():
-                stage_a(0)
-
-            def far(jm):
+                for i in range(nz - 2):
+                    stage_end(i)
+                if 1 < min(ahead, n):
+                    y_send(1)
+                for i in range(nz - 2, nz):
+                    og_to_peers(i)
+                for c in range(2, min(ahead, n)):
+                    y_send(c)
+                for i in range(nz - 2):
+                    stage_a(i)
+                stage_c(0)
+
+            @pl.when(jnp.logical_and(first >= 0, first < n))
+            def _():
+                def took_hidden(count):
+                    arrived(h.at[first, pl.ds(0, count * tokens)], h_sem.at[first])
+
+                if half == 2:
+                    took_hidden(slots)
+                else:
+                    pl.when(zm == 1)(functools.partial(took_hidden, slots))
+                    pl.when(zm > 1)(functools.partial(took_hidden, ny))
+
+                @pl.when(first + ahead < n)
+                def _():
+                    y_send(first + ahead)
+
+            def far(jm, f):
                 j = mirrored(jm)
-
-                def go():
-                    own = partial(j, f)
-                    if half == 2:
+                own = partial(j, f)
+                if half == 2:
+                    send[j, f] = own.astype(BF16)
+                else:
+                    @pl.when(zm == 1)
+                    def _():
                         send[j, f] = own.astype(BF16)
-                    else:
-                        @pl.when(zm == 1)
-                        def _():
-                            send[j, f] = own.astype(BF16)
-
-                        @pl.when(zm > 1)
-                        def _():
-                            took(far_slot(j), f)
-                            send[j, f] = (own + recv[far_slot(j), f].astype(F32)).astype(BF16)
-
-                    remote(
-                        send.at[j, f], recv.at[far_slot(j), f],
-                        s_send.at[j], recv_sem.at[far_slot(j), f], at(z + toward, y),
-                    )
-
-                if jm >= half:
-                    pl.when(f_on)(go)
-                else:
-                    pl.when(jnp.logical_and(f_on, jm > zm))(go)
-
-            for i in range(nz - 2):
-                @pl.when(s == 0)
-                def _():
-                    stage_a(i + 1)
+
+                    @pl.when(zm > 1)
+                    def _():
+                        took(far_slot(jm), f)
+                        send[j, f] = (own + recv[far_slot(jm), f].astype(F32)).astype(BF16)
+
+                remote(
+                    send.at[j, f], recv.at[onward_slot(jm), f],
+                    s_send.at[j], recv_sem.at[onward_slot(jm), f], at(z + toward, y),
+                )
+
+            @pl.when(jnp.logical_and(first >= 0, first < n))
+            def _():
+                far(nz - 1, first)
+
+
+            @pl.when(s == 1)
+            def _():
+                for i in range(1, nz - 2):
                     stage_b(i)
                     stage_c(i)
 
-                if i == 0:
-                    @pl.when(f_on)
-                    def _():
-                        arrived(h.at[f, block(y, tokens)], h_sem.at[y, f])
-                        each_slot(lambda slot: arrived(h.at[f, block(slot, tokens)], h_sem.at[slot, f]))
-
-                        @pl.when(f + ahead < n)
-                        def _():
-                            y_send(f + ahead)
-
-                far(nz - 1 - i)
-
-            @pl.when(s == 1)
-            def _():
-                stage_a(nz - 1)
+            def done_later(v):
+                return jnp.clip(jnp.where(v < 2, v, v + 1), 0, n)
+
+            def later(f, carry):
+                for jm in range(nz - 2, 1, -1):
+                    if jm >= half:
+                        far(jm, f)
+                    else:
+                        pl.when(jm > zm)(functools.partial(far, jm, f))
+                return carry
+
+            lax.fori_loop(done_later(first - 1), done_later(first), later, 0)
+
+            @pl.when(s == 2)
+            def _():
+                for i in range(nz - 2, nz):
+                    stage_end(i)
+
+            @pl.when(s == 3)
+            def _():
+                for i in range(nz - 2, nz):
+                    stage_a(i)
+
+            @pl.when(s == 4)
+            def _():
                 for i in range(nz - 2, nz):
                     stage_b(i)
+
+            @pl.when(s == late - 1)
+            def _():
+                for i in range(nz - 2, nz):
                     stage_c(i)
-
-            c = s - (nz - 2 - inner_z) * lag
-
-            @pl.when(jnp.logical_and(c >= 0, c < n))
-            def _():
+                pltpu.make_async_copy(mom_hbm, mom, mom_sem).wait()
+                pltpu.make_async_copy(sec_hbm, sec_ref, sec_sem).wait()
+
+            near_lag = (nz - 2 - inner_z) * lag
+
+            def done_near(v):
+                return jnp.clip(jnp.minimum(2 * (v + 1 - late), v + 1 - near_lag), 0, n)
+
+            def near_chunk(c, carry):
                 def near(jm):
                     j = mirrored(jm)
                     own = partial(j, c)
-                    took(near_slot(j), c)
-                    send[j, c] = (own + recv[near_slot(j), c].astype(F32)).astype(BF16)
+                    took(jm, c)
+                    send[j, c] = (own + recv[jm, c].astype(F32)).astype(BF16)
 
                     def to_end():
                         for k in range(ny):
                             p = lax.rem(y + 1 + k, ny)
                             remote(
-                                send.at[j, c, block(p, rows)], fin.at[y, c],
-                                s_send.at[j], fin_sem.at[y, c], at(z_end, p),
+                                send.at[j, c, block(p, rows)], fin.at[c, y],
+                                s_send.at[j], fin_sem.at[c], at(z_end, p),
                             )
 
                     def onward():
                         remote(
-                            send.at[j, c], recv.at[near_slot(j), c],
-                            s_send.at[j], recv_sem.at[near_slot(j), c], at(z - toward, y),
+                            send.at[j, c], recv.at[jm, c],
+                            s_send.at[j], recv_sem.at[jm, c], at(z - toward, y),
                         )
 
                     if jm > 0:
@@ -443,30 +507,30 @@
                         pl.when(jm < zm)(functools.partial(near, jm))
 
                 acc[...] = partial(z, c)
-                took(near_slot(z), c)
-                acc[...] += recv[near_slot(z), c].astype(F32)
+                took(inner_z, c)
+                acc[...] += recv[inner_z, c].astype(F32)
                 if half > 2:
                     @pl.when(zm > 1)
                     def _():
-                        took(far_slot(z), c)
-                        acc[...] += recv[far_slot(z), c].astype(F32)
+                        took(far_slot(zm), c)
+                        acc[...] += recv[far_slot(zm), c].astype(F32)
 
                 for k in range(1, ny):
                     p = lax.rem(y + k, ny)
                     send[z, c, block(p, rows)] = acc[block(p, rows)].astype(BF16)
                     remote(
-                        send.at[z, c, block(p, rows)], fin.at[y, c],
-                        s_send.at[z], fin_sem.at[y, c], at_y(k),
+                        send.at[z, c, block(p, rows)], fin.at[c, y],
+                        s_send.at[z], fin_sem.at[c], at_y(k),
                     )
                 process(y * n + c, acc[block(y, rows)])
-
-            g = c - fin_lag
-
-            @pl.when(jnp.logical_and(g >= 0, g < n))
-            def _():
-                for k in range(1, ny):
-                    process_fin(lax.rem(y + k, ny), g)
-
+                return carry
+
+            def fin_chunk(c, carry):
+                process_fin(ny - 1, c)
+                return carry
+
+            lax.fori_loop(done_near(s - 1), done_near(s), near_chunk, 0)
+            lax.fori_loop(done_near(s - 1 - fin_lag), done_near(s - fin_lag), fin_chunk, 0)
             return carry
 
         lax.fori_loop(0, steps, step, 0)
@@ -511,23 +575,33 @@
 
     blocks = h.at[:, pl.ds(0, tokens)]
 
-    def og_sent(k):
-        sent(ograw.at[0, pl.ds(0, tokens // 2), pl.ds(0, group)], og_send.at[0, k])
-        sent(ograw.at[0, pl.ds(0, tau), pl.ds(0, (nz - 1) * group)], og_send.at[1, k])
+    def og_sent(sems, k):
+        sent(ograw.at[0, pl.ds(0, tokens // 2), pl.ds(0, group)], sems.at[0, k])
+        sent(ograw.at[0, pl.ds(0, tau), pl.ds(0, (nz - 1) * group)], sems.at[1, k])
 
     for k in range(1, ny):
         sent(blocks, hy_send.at[k - 1])
-        og_sent(k)
 
     @pl.when(is_end)
     def _():
-        og_sent(0)
+        og_sent(og_send, 0)
         sent(blocks, end_send)
         for k in range(1, ny):
             sent(blocks, fwd_send.at[k - 1])
 
     @pl.when(jnp.logical_not(is_end))
     def _():
+        def og_forwarded():
+            for k in range(1, ny):
+                og_sent(ogy_send, k - 1)
+
+        for k in range(1, ny):
+            og_sent(og_send, k)
+        if half == 2:
+            og_forwarded()
+        else:
+            pl.when(zm == 1)(og_forwarded)
+
         def og_gather(count):
             pieces = ograw.at[pl.ds(0, count), pl.ds(0, tau), pl.ds(0, (nz - 1) * group)]
             sent(ograw.at[pl.ds(0, count), pl.ds(0, tokens // 2), pl.ds(0, group)], ogc_send.at[0, 0])
@@ -580,6 +654,7 @@
     width = 128
     n = part // width
     group = ny * rows
+    recv_slots = nz // 2 if nz == 4 else nz // 2 + nz
     dma = pltpu.SemaphoreType.DMA
     anywhere = pl.BlockSpec(memory_space=pltpu.HBM)
     vmem = pl.BlockSpec(memory_space=pltpu.VMEM)
@@ -597,18 +672,19 @@
             pltpu.VMEM((n, 2 * ny * tokens, width), BF16),
             pltpu.VMEM((2 * ny, tokens, nz * group), BF16),
             pltpu.VMEM((nz if nz == 4 else 1, group, 2 * ny * tokens), BF16),
-            pltpu.VMEM((nz + 1, n, group, width), BF16),
+            pltpu.VMEM((recv_slots, n, group, width), BF16),
             pltpu.VMEM((nz, n, group, width), BF16),
-            pltpu.VMEM((ny, n, rows, width), BF16),
+            pltpu.VMEM((n, ny, rows, width), BF16),
             pltpu.VMEM((group, width), F32),
             pltpu.VMEM((rows, rows), F32),
             pltpu.VMEM((nt, rows, rows), BF16),
             pltpu.VMEM((1, rows), F32),
-            dma((2 * ny, n)),
+            dma((n,)),
             dma((2 * ny, nz, nt)),
             dma,
-            dma((nz + 1, n)),
-            dma((ny, n)),
+            dma((2, max(ny - 1, 1))),
+            dma((recv_slots, n)),
+            dma((n,)),
             dma,
             dma,
             dma((max(ny - 1, 1),)),

time: 116 us -> 110 us (0.948)
  Pallas kernels: 115 us -> 109 us
    pallas_call x1, Pallas kernels: 112 us -> 106 us  [body(): pl.pallas_call(functools.partial(kernel, nz, ny, nt, n, float(cols * nt))...]
where the time goes in v3:
time: 110 us
  Pallas kernels  109 us (99%)
    pallas_call x1, Pallas kernels, body(): pl.pallas_call(functools.partial(kernel, nz, ny, nt, n, float(cols * nt))...  106 us
    pallas_call x1, Pallas kernels, body(): pl.pallas_call(write_kernel, out_shape=(jax.ShapeDtypeStruct((rows, cols)...  3.67 us

profile of v3, /device:TPU:0, one launch (start us, length us, event | category | flops | bytes accessed | tf_op | source)
XLA Modules:
  0.0 109.9 jit_solution(15282798666488344716)
XLA Ops:
  0.6 105.6 %normuon.1 = (bf16[128,7168]{1,0:T(8,128)(2,1)S(1)}, f32[128,7168]{1,0:T(8,128)S(1)}, f32[128,128]{1,0:T(8,128)S(1)}, f32[1,128]{1,0:T(1,128)S(1)}) custom-call(bf16[256,1024]{1,0:T(8,128)(2,1)} %og_hbm.1, bf16[256,7168]{1,0:T(8,128)(2,1)} %h_hbm.1, f32[128,7168]{1,0:T(8,128)} %mom_hbm.1, f32[1,128]{1,0:T(1,128)} %bitcast.2), custom_call_target="tpu_custom_call" | custom-call | tf_op jit(solution)/shard_map/normuon/pallas_call | solution.py:661
  106.2 3.7 %write_results.1 = (bf16[128,7168]{1,0:T(8,128)(2,1)}, f32[128,7168]{1,0:T(8,128)}, f32[1,128]{1,0:T(1,128)}) custom-call(bf16[128,7168]{1,0:T(8,128)(2,1)S(1)} %get-tuple-element.10.x, f32[128,7168]{1,0:T(8,128)S(1)} %get-tuple-element.11.mom, f32[128,128]{1,0:T(8,128)S(1)} %get-tuple-element.12.final_ref, f32[1,128]{1,0:T(1,128)S(1)} %get-tuple-element.13.sec_ref), custom_call_target="tpu_custom_call" | custom-call | tf_op jit(solution)/shard_map/write_results/pallas_call | solution.py:710

commit v4 on v3

--- a/solution.py
+++ b/solution.py
@@ -26,16 +26,16 @@
     return n_dp // ny, ny
 
 
-def exact_dot(a, b):
-    return jnp.dot(a, b, preferred_element_type=F32, precision=lax.Precision.HIGHEST)
+def small_dot(a, b):
+    return jnp.dot(a.astype(BF16), b.astype(BF16), preferred_element_type=F32)
 
 
 def kernel(
     nz, ny, nt, n, ff,
     og_hbm, h_hbm, mom_hbm, sec_hbm,
     x, mom, final_ref, secout_ref,
-    h, ograw, og_t, recv, send, fin, acc, gram, g_all, sec_ref,
-    h_sem, og_sem, og_own, ogy_send, recv_sem, fin_sem, mom_sem, sec_sem,
+    h, ograw, og_t, recv, send, fin, acc, kept, cross, gram, g_all, sec_ref,
+    h_sem, og_sem, og_own, ogy_send, recv_sem, cross_sem, fin_sem, mom_sem, sec_sem,
     hy_send, end_send, fwd_send, og_send, ogx_send, ogc_send, s_send, g_send, g_recv,
 ):
     tokens, part = h_hbm.shape[0], h_hbm.shape[1] // ny
@@ -45,7 +45,7 @@
     nx = nt // 2
     slots = 2 * ny
     half = nz // 2
-    ahead, end_ahead, lag, late, fin_lag = nz + 1, 1, 2, 6, 2
+    ahead, end_ahead, lag, late, fin_lag = nz + 1, 1, 1, 9, 2
     d = lax.axis_index("dp")
     t = lax.axis_index("tensor")
     z, y = d // ny, lax.rem(d, ny)
@@ -97,6 +97,9 @@
         return block(p * n + c, width)
 
     inner_z = 1 if half == 2 else zm
+    direct = half == 2
+    tail = kept.shape[0]
+    streamed = n - tail if direct else n
     z_end = jnp.where(lower, 0, nz - 1)
 
     barrier = pltpu.get_barrier_semaphore()
@@ -113,10 +116,17 @@
     def _():
         for k in range(ny):
             hello(at(z + toward, k))
+            if direct:
+                hello(at(z + 2 * toward, k))
 
     @pl.when(jnp.logical_not(is_end))
     def _():
-        hello(at(z + toward, y))
+        if direct:
+            for k in range(ny):
+                hello(at(z + toward, k))
+                hello(at(z + 2 * toward, k))
+        else:
+            hello(at(z + toward, y))
 
         def ends():
             for k in range(ny):
@@ -134,7 +144,11 @@
     greeted = (ny - 1) + (nt - 1)
     pl.semaphore_wait(
         barrier,
-        greeted + jnp.where(zm == 0, ny, 0) + jnp.where(zm == 1, ny + 1, 0) + jnp.where(zm > 1, 2, 0),
+        greeted
+        + (
+            jnp.where(is_end, 2 * ny, 3 * ny) if direct
+            else jnp.where(zm == 0, ny, 0) + jnp.where(zm == 1, ny + 1, 0) + jnp.where(zm > 1, 2, 0)
+        ),
     )
 
     def share(i, tt):
@@ -173,6 +187,13 @@
             p = lax.rem(y + k, ny)
             process(p * n + c, fin[c, p].astype(F32))
 
+    def process_last(count, i):
+        arrived(fin.at[streamed + i, pl.ds(0, count)], fin_sem.at[streamed + i])
+        for k in range(ny - count, ny):
+            p = lax.rem(y + k, ny)
+            arrived(cross.at[i, p], cross_sem.at[i, p])
+            process(p * n + streamed + i, fin[streamed + i, p].astype(F32) + cross[i, p].astype(F32))
+
     @pl.when(is_end)
     def _():
         z_in = z + toward
@@ -219,7 +240,7 @@
             def _():
                 own_to_inner(c + end_ahead)
 
-            @pl.when(c == min(2, n) - 1)
+            @pl.when(c == min(late - 4, n) - 1)
             def _():
                 for i in range(nz - 2, nz):
                     og_to_inner(i)
@@ -234,7 +255,10 @@
             process_fin(ny, c)
             return carry
 
-        lax.fori_loop(0, n, finish, 0)
+        lax.fori_loop(0, streamed, finish, 0)
+        if direct:
+            for i in range(tail):
+                process_last(ny, i)
 
     @pl.when(jnp.logical_not(is_end))
     def _():
@@ -416,10 +440,24 @@
                         took(far_slot(jm), f)
                         send[j, f] = (own + recv[far_slot(jm), f].astype(F32)).astype(BF16)
 
-                remote(
-                    send.at[j, f], recv.at[onward_slot(jm), f],
-                    s_send.at[j], recv_sem.at[onward_slot(jm), f], at(z + toward, y),
-                )
+                def onward():
+                    remote(
+                        send.at[j, f], recv.at[onward_slot(jm), f],
+                        s_send.at[j], recv_sem.at[onward_slot(jm), f], at(z + toward, y),
+                    )
+
+                if not direct:
+                    onward()
+                    return
+                pl.when(f < streamed)(onward)
+
+                @pl.when(f >= streamed)
+                def _():
+                    for p in range(ny):
+                        remote(
+                            send.at[j, f, pl.ds(p * rows, rows)], cross.at[f - streamed, y],
+                            s_send.at[j], cross_sem.at[f - streamed, y], at(j, p),
+                        )
 
             @pl.when(jnp.logical_and(first >= 0, first < n))
             def _():
@@ -445,17 +483,17 @@
 
             lax.fori_loop(done_later(first - 1), done_later(first), later, 0)
 
-            @pl.when(s == 2)
+            @pl.when(s == late - 5)
             def _():
                 for i in range(nz - 2, nz):
                     stage_end(i)
 
-            @pl.when(s == 3)
+            @pl.when(s == late - 4)
             def _():
                 for i in range(nz - 2, nz):
                     stage_a(i)
 
-            @pl.when(s == 4)
+            @pl.when(s == late - 3)
             def _():
                 for i in range(nz - 2, nz):
                     stage_b(i)
@@ -469,8 +507,37 @@
 
             near_lag = (nz - 2 - inner_z) * lag
 
+            def to_end(j, c):
+                for k in range(ny):
+                    p = lax.rem(y + 1 + k, ny)
+                    remote(
+                        send.at[j, c, block(p, rows)], fin.at[c, y],
+                        s_send.at[j], fin_sem.at[c], at(z_end, p),
+                    )
+
+            def to_peers(c):
+                for k in range(1, ny):
+                    p = lax.rem(y + k, ny)
+                    send[z, c, block(p, rows)] = acc[block(p, rows)].astype(BF16)
+                    remote(
+                        send.at[z, c, block(p, rows)], fin.at[c, y],
+                        s_send.at[z], fin_sem.at[c], at_y(k),
+                    )
+
+            if direct:
+                own = s - max(late - streamed, 0)
+
+                @pl.when(jnp.logical_and(own >= streamed, own < n))
+                def _():
+                    send[z_end, own] = partial(z_end, own).astype(BF16)
+                    to_end(z_end, own)
+                    acc[...] = partial(z, own)
+                    to_peers(own)
+                    kept[own - streamed] = acc[block(y, rows)]
+
+
             def done_near(v):
-                return jnp.clip(jnp.minimum(2 * (v + 1 - late), v + 1 - near_lag), 0, n)
+                return jnp.clip(jnp.minimum(2 * (v + 1 - late), v + 1 - near_lag), 0, streamed)
 
             def near_chunk(c, carry):
                 def near(jm):
@@ -479,14 +546,6 @@
                     took(jm, c)
                     send[j, c] = (own + recv[jm, c].astype(F32)).astype(BF16)
 
-                    def to_end():
-                        for k in range(ny):
-                            p = lax.rem(y + 1 + k, ny)
-                            remote(
-                                send.at[j, c, block(p, rows)], fin.at[c, y],
-                                s_send.at[j], fin_sem.at[c], at(z_end, p),
-                            )
-
                     def onward():
                         remote(
                             send.at[j, c], recv.at[jm, c],
@@ -496,7 +555,7 @@
                     if jm > 0:
                         onward()
                     else:
-                        when(near_end, to_end)
+                        when(near_end, functools.partial(to_end, j, c))
                         if half > 2:
                             pl.when(zm > 1)(onward)
 
@@ -515,13 +574,7 @@
                         took(far_slot(zm), c)
                         acc[...] += recv[far_slot(zm), c].astype(F32)
 
-                for k in range(1, ny):
-                    p = lax.rem(y + k, ny)
-                    send[z, c, block(p, rows)] = acc[block(p, rows)].astype(BF16)
-                    remote(
-                        send.at[z, c, block(p, rows)], fin.at[c, y],
-                        s_send.at[z], fin_sem.at[c], at_y(k),
-                    )
+                to_peers(c)
                 process(y * n + c, acc[block(y, rows)])
                 return carry
 
@@ -534,6 +587,11 @@
             return carry
 
         lax.fori_loop(0, steps, step, 0)
+        if direct:
+            for i in range(tail):
+                arrived(cross.at[i, y], cross_sem.at[i, y])
+                process(y * n + streamed + i, kept[i] + cross[i, y].astype(F32))
+                process_last(ny - 1, i)
 
     g_all[t] = gram[...].astype(BF16)
     for k in range(1, nt):
@@ -557,12 +615,12 @@
     current = summed * inverse * inverse
     map_all = None
     for iteration in range(ITERS):
-        square = exact_dot(current, current)
+        square = small_dot(current, current)
         map_one = quintic_a * eye + quintic_b * current + quintic_c * square
-        map_all = map_one if map_all is None else exact_dot(map_one, map_all)
-        mapped = exact_dot(map_one, current)
+        map_all = map_one if map_all is None else small_dot(map_one, map_all)
+        mapped = small_dot(map_one, current)
         if iteration < ITERS - 1:
-            current = exact_dot(mapped, map_one)
+            current = small_dot(mapped, map_one)
     energy = jnp.sum(mapped * map_one, axis=0, keepdims=True)
     second_out = beta_two * sec_ref[...] + (1.0 - beta_two) * energy
     secout_ref[...] = second_out
@@ -629,11 +687,13 @@
 
 
 def write_kernel(x, mom, final_ref, sec_ref, upd_hbm, momout_hbm, secout_ref, out, mom_sem, upd_sem):
-    pltpu.make_async_copy(mom, momout_hbm, mom_sem).start()
+    for r in range(4):
+        band = pl.ds(r * (mom.shape[0] // 4), mom.shape[0] // 4)
+        pltpu.make_async_copy(mom.at[band], momout_hbm.at[band], mom_sem).start()
     high = final_ref[...].astype(BF16)
     secout_ref[...] = sec_ref[...]
     cols = x.shape[1]
-    width = 512 if cols % 512 == 0 else 128
+    width = 1024 if cols % 1024 == 0 else 512 if cols % 512 == 0 else 128
     n = cols // width
 
     def finish(c, carry):
@@ -654,6 +714,7 @@
     width = 128
     n = part // width
     group = ny * rows
+    tail = min(2, n)
     recv_slots = nz // 2 if nz == 4 else nz // 2 + nz
     dma = pltpu.SemaphoreType.DMA
     anywhere = pl.BlockSpec(memory_space=pltpu.HBM)
@@ -676,6 +737,8 @@
             pltpu.VMEM((nz, n, group, width), BF16),
             pltpu.VMEM((n, ny, rows, width), BF16),
             pltpu.VMEM((group, width), F32),
+            pltpu.VMEM((tail, rows, width), F32),
+            pltpu.VMEM((tail, ny, rows, width), BF16),
             pltpu.VMEM((rows, rows), F32),
             pltpu.VMEM((nt, rows, rows), BF16),
             pltpu.VMEM((1, rows), F32),
@@ -684,6 +747,7 @@
             dma,
             dma((2, max(ny - 1, 1))),
             dma((recv_slots, n)),
+            dma((tail, ny)),
             dma((n,)),
             dma,
             dma,

time: 110 us -> 107 us (0.973)
  Pallas kernels: 109 us -> 107 us
    pallas_call x1, Pallas kernels: 106 us -> 104 us  [body(): pl.pallas_call(functools.partial(kernel, nz, ny, nt, n, float(cols * nt))...]
where the time goes in v4:
time: 107 us
  Pallas kernels  107 us (100%)
    pallas_call x1, Pallas kernels, body(): pl.pallas_call(functools.partial(kernel, nz, ny, nt, n, float(cols * nt))...  104 us
    pallas_call x1, Pallas kernels, body(): pl.pallas_call(write_kernel, out_shape=(jax.ShapeDtypeStruct((rows, cols)...  2.93 us

profile of v4, /device:TPU:0, one launch (start us, length us, event | category | flops | bytes accessed | tf_op | source)
XLA Modules:
  0.0 107.1 jit_solution(2096688329510365920)
XLA Ops:
  0.6 103.6 %normuon.1 = (bf16[128,7168]{1,0:T(8,128)(2,1)S(1)}, f32[128,7168]{1,0:T(8,128)S(1)}, f32[128,128]{1,0:T(8,128)S(1)}, f32[1,128]{1,0:T(1,128)S(1)}) custom-call(bf16[256,1024]{1,0:T(8,128)(2,1)} %og_hbm.1, bf16[256,7168]{1,0:T(8,128)(2,1)} %h_hbm.1, f32[128,7168]{1,0:T(8,128)} %mom_hbm.1, f32[1,128]{1,0:T(1,128)} %bitcast.2), custom_call_target="tpu_custom_call" | custom-call | tf_op jit(solution)/shard_map/normuon/pallas_call | solution.py:722
  104.2 2.9 %write_results.1 = (bf16[128,7168]{1,0:T(8,128)(2,1)}, f32[128,7168]{1,0:T(8,128)}, f32[1,128]{1,0:T(1,128)}) custom-call(bf16[128,7168]{1,0:T(8,128)(2,1)S(1)} %get-tuple-element.10.x, f32[128,7168]{1,0:T(8,128)S(1)} %get-tuple-element.11.mom, f32[128,128]{1,0:T(8,128)S(1)} %get-tuple-element.12.final_ref, f32[1,128]{1,0:T(1,128)S(1)} %get-tuple-element.13.sec_ref), custom_call_target="tpu_custom_call" | custom-call | tf_op jit(solution)/shard_map/write_results/pallas_call | solution.py:774

commit v5 on v4

--- a/solution.py
+++ b/solution.py
@@ -202,7 +202,7 @@
             j = mirrored(nz - 1 - i)
             remote(
                 og_hbm.at[share(i, t), rows_of(j)], ograw.at[ny + y, share(i, t), rows_of(j)],
-                og_send.at[min(i, 1), 0], og_sem.at[ny + y, j, t], at(z_in, y),
+                og_send.at[min(i, 1), 0], og_sem.at[i, ny + y], at(z_in, y),
             )
 
         def own_to_inner(c):
@@ -268,7 +268,7 @@
             for k in range(1, ny):
                 remote(
                     og_hbm.at[share(i, t), rows_of(j)], ograw.at[y, share(i, t), rows_of(j)],
-                    og_send.at[min(i, 1), k], og_sem.at[y, j, t], at_y(k),
+                    og_send.at[min(i, 1), k], og_sem.at[i, y], at_y(k),
                 )
 
         og_to_peers(0)
@@ -314,29 +314,38 @@
         def to_core(i, slot, tt, k):
             remote(
                 og_piece(i, slot, tt), og_piece(i, slot, tt), ogc_send.at[min(i, 1), k],
-                og_sem.at[slot, mirrored(nz - 1 - i), tt], at_t(tx * 2 + 1 - core),
+                og_sem.at[i, slots + nx], at_t(tx * 2 + 1 - core),
             )
 
-        def og_took(i, slot, tt):
-            arrived(og_piece(i, slot, tt), og_sem.at[slot, mirrored(nz - 1 - i), tt])
+        def og_took(i, slot):
+            arrived(og_piece(i, slot, t), og_sem.at[i, slot])
+
+        def og_gathered(i, sem, share_rows):
+            def took_all(count):
+                arrived(ograw.at[pl.ds(0, count), pl.ds(0, share_rows), pl.ds(0, group)], og_sem.at[i, sem])
+
+            if half == 2:
+                took_all(slots - 1)
+            else:
+                pl.when(zm == 1)(functools.partial(took_all, slots - 1))
+                pl.when(zm > 1)(functools.partial(took_all, ny - 1))
 
         def share_out(i, slot):
             if i > 0:
                 for k in range(1, nx):
                     remote(
                         og_piece(i, slot, t), og_piece(i, slot, t), ogx_send.at[k - 1],
-                        og_sem.at[slot, mirrored(nz - 1 - i), t],
-                        at_t(lax.rem(tx + k, nx) * 2 + core),
+                        og_sem.at[i, slots + tx], at_t(lax.rem(tx + k, nx) * 2 + core),
                     )
             to_core(i, slot, t, 0)
 
         def stage_end(i):
             def go():
-                og_took(i, ny + y, t)
+                og_took(i, ny + y)
                 for k in range(1, ny):
                     remote(
                         og_piece(i, ny + y, t), og_piece(i, ny + y, t), ogy_send.at[min(i, 1), k - 1],
-                        og_sem.at[ny + y, mirrored(nz - 1 - i), t], at_y(k),
+                        og_sem.at[i, ny + y], at_y(k),
                     )
                 share_out(i, ny + y)
 
@@ -344,32 +353,22 @@
 
         def stage_a(i):
             def one(slot):
-                og_took(i, slot, t)
+                og_took(i, slot)
                 share_out(i, slot)
 
             peer_slots(one)
 
         def stage_b(i):
-            def one(slot):
-                for k in range(1, nx):
-                    tt = lax.rem(tx + k, nx) * 2 + core
-                    og_took(i, slot, tt)
-                    to_core(i, slot, tt, k)
-
-            if i > 0:
-                each_slot(one)
+            if i == 0:
+                return
+            for k in range(1, nx):
+                ox = lax.rem(tx + k, nx)
+                og_gathered(i, slots + ox, tau)
+                each_slot(lambda slot: to_core(i, slot, ox * 2 + core, k))
 
         def stage_c(i):
             j = mirrored(nz - 1 - i)
-
-            def one(slot):
-                if i == 0:
-                    og_took(i, slot, tx * 2 + 1 - core)
-                else:
-                    for k in range(nx):
-                        og_took(i, slot, k * 2 + 1 - core)
-
-            each_slot(one)
+            og_gathered(i, slots + nx, tokens // 2)
             for slot in range(slots if half == 2 else 0):
                 for r in range(ny):
                     og_t[j, r * rows : (r + 1) * rows, slot * tokens : (slot + 1) * tokens] = (
@@ -389,7 +388,7 @@
             return jnp.dot(og_t[j], h[c], preferred_element_type=F32)
 
         def took(idx, c):
-            arrived(recv.at[idx, c], recv_sem.at[idx, c])
+            arrived(recv.at[c, idx], recv_sem.at[idx, c])
 
         steps = n + max((nz - 3) * lag, late) + fin_lag
 
@@ -438,11 +437,11 @@
                     @pl.when(zm > 1)
                     def _():
                         took(far_slot(jm), f)
-                        send[j, f] = (own + recv[far_slot(jm), f].astype(F32)).astype(BF16)
+                        send[j, f] = (own + recv[f, far_slot(jm)].astype(F32)).astype(BF16)
 
                 def onward():
                     remote(
-                        send.at[j, f], recv.at[onward_slot(jm), f],
+                        send.at[j, f], recv.at[f, onward_slot(jm)],
                         s_send.at[j], recv_sem.at[onward_slot(jm), f], at(z + toward, y),
                     )
 
@@ -459,7 +458,7 @@
                             s_send.at[j], cross_sem.at[f - streamed, y], at(j, p),
                         )
 
-            @pl.when(jnp.logical_and(first >= 0, first < n))
+            @pl.when(jnp.logical_and(first >= 0, first < (streamed if direct else n)))
             def _():
                 far(nz - 1, first)
 
@@ -482,6 +481,11 @@
                 return carry
 
             lax.fori_loop(done_later(first - 1), done_later(first), later, 0)
+
+            if direct:
+                @pl.when(jnp.logical_and(first >= streamed, first < n))
+                def _():
+                    far(nz - 1, first)
 
             @pl.when(s == late - 5)
             def _():
@@ -544,11 +548,11 @@
                     j = mirrored(jm)
                     own = partial(j, c)
                     took(jm, c)
-                    send[j, c] = (own + recv[jm, c].astype(F32)).astype(BF16)
+                    send[j, c] = (own + recv[c, jm].astype(F32)).astype(BF16)
 
                     def onward():
                         remote(
-                            send.at[j, c], recv.at[jm, c],
+                            send.at[j, c], recv.at[c, jm],
                             s_send.at[j], recv_sem.at[jm, c], at(z - toward, y),
                         )
 
@@ -567,12 +571,12 @@
 
                 acc[...] = partial(z, c)
                 took(inner_z, c)
-                acc[...] += recv[inner_z, c].astype(F32)
+                acc[...] += recv[c, inner_z].astype(F32)
                 if half > 2:
                     @pl.when(zm > 1)
                     def _():
                         took(far_slot(zm), c)
-                        acc[...] += recv[far_slot(zm), c].astype(F32)
+                        acc[...] += recv[c, far_slot(zm)].astype(F32)
 
                 to_peers(c)
                 process(y * n + c, acc[block(y, rows)])
@@ -733,7 +737,7 @@
             pltpu.VMEM((n, 2 * ny * tokens, width), BF16),
             pltpu.VMEM((2 * ny, tokens, nz * group), BF16),
             pltpu.VMEM((nz if nz == 4 else 1, group, 2 * ny * tokens), BF16),
-            pltpu.VMEM((recv_slots, n, group, width), BF16),
+            pltpu.VMEM((n, recv_slots, group, width), BF16),
             pltpu.VMEM((nz, n, group, width), BF16),
             pltpu.VMEM((n, ny, rows, width), BF16),
             pltpu.VMEM((group, width), F32),
@@ -743,7 +747,7 @@
             pltpu.VMEM((nt, rows, rows), BF16),
             pltpu.VMEM((1, rows), F32),
             dma((n,)),
-            dma((2 * ny, nz, nt)),
+            dma((nz, 2 * ny + nt // 2 + 1)),
             dma,
             dma((2, max(ny - 1, 1))),
             dma((recv_slots, n)),

time: 107 us -> 107 us (level)
  no operation moved by 1% of the time
where the time goes in v5:
time: 107 us; the launch traced here: 106 us
  Pallas kernels  106 us (99%)
    pallas_call x1, Pallas kernels, body(): pl.pallas_call(functools.partial(kernel, nz, ny, nt, n, float(cols * nt))...  103 us
    pallas_call x1, Pallas kernels, body(): pl.pallas_call(write_kernel, out_shape=(jax.ShapeDtypeStruct((rows, cols)...  2.93 us

profile of v5, /device:TPU:0, one launch (start us, length us, event | category | flops | bytes accessed | tf_op | source)
XLA Modules:
  0.0 106.4 jit_solution(11885507075073678089)
XLA Ops:
  0.6 102.8 %normuon.1 = (bf16[128,7168]{1,0:T(8,128)(2,1)S(1)}, f32[128,7168]{1,0:T(8,128)S(1)}, f32[128,128]{1,0:T(8,128)S(1)}, f32[1,128]{1,0:T(1,128)S(1)}) custom-call(bf16[256,1024]{1,0:T(8,128)(2,1)} %og_hbm.1, bf16[256,7168]{1,0:T(8,128)(2,1)} %h_hbm.1, f32[128,7168]{1,0:T(8,128)} %mom_hbm.1, f32[1,128]{1,0:T(1,128)} %bitcast.2), custom_call_target="tpu_custom_call" | custom-call | tf_op jit(solution)/shard_map/normuon/pallas_call | solution.py:726
  103.5 2.9 %write_results.1 = (bf16[128,7168]{1,0:T(8,128)(2,1)}, f32[128,7168]{1,0:T(8,128)}, f32[1,128]{1,0:T(1,128)}) custom-call(bf16[128,7168]{1,0:T(8,128)(2,1)S(1)} %get-tuple-element.10.x, f32[128,7168]{1,0:T(8,128)S(1)} %get-tuple-element.11.mom, f32[128,128]{1,0:T(8,128)S(1)} %get-tuple-element.12.final_ref, f32[1,128]{1,0:T(1,128)S(1)} %get-tuple-element.13.sec_ref), custom_call_target="tpu_custom_call" | custom-call | tf_op jit(solution)/shard_map/write_results/pallas_call | solution.py:778
